TPU v7x, 256 devices: a whole 4x4x8 slice. The times are simulated.
256 devices in a mesh: replica: 8 (over y, x_lo), fsdp: 32 (over z, x_hi, core).
Axes of the slice: x: 4 (x_hi: 2, x_lo: 2; x = x_hi * 2 + x_lo), y: 4, z: 8, core: 2. Of those that a mesh axis runs over, the one named last changes fastest.
Arguments:
- local_weights: bfloat16 [8, 1024, 28672], P('replica', 'fsdp'), may hold values from -6 to 6
- base_weights: float32 [1024, 28672], P('fsdp'), may hold values from -6 to 6
- momentum: float32 [1024, 28672], P('replica', 'fsdp'), may hold values from -4 to 4
Outputs:
- new_weights: float32 [1024, 28672], P('fsdp')
- new_momentum: float32 [1024, 28672], P('replica', 'fsdp')
All inputs are finite; a program needn't handle non-finite values. Where the computation divides by a largest or mean magnitude, that divisor is 1e-20 or more.
Results may differ from a plain program's by a relative error of at most 0.015.
Values may be sent and summed in bfloat16 or wider, within the bound.
No kernel may reach another device: no remote copies, remote signals or barrier semaphores. Data moves between devices by JAX's collectives and lax.ppermute only.
A program may use at most 128 MiB of HBM per device.

v0:
```python
import jax
import jax.numpy as jnp
from jax import lax
from jax.sharding import Mesh
from jax.sharding import PartitionSpec as P

QBLOCK = 128
FSDP = ("fsdp_0", "fsdp_1", "fsdp_2")


EPSILON = 1e-06
LEARN_RATE = 0.7
MOMENTUM_COEF = 0.9


def cut_along(array, dim, size):
    shape = array.shape
    parts = array.reshape(*shape[:dim], size, shape[dim] // size, *shape[dim + 1 :])
    return jnp.moveaxis(parts, dim, 0)


def laid_out(parts, dim):
    parts = jnp.moveaxis(parts, 0, dim)
    shape = parts.shape
    return parts.reshape(*shape[:dim], shape[dim] * shape[dim + 1], *shape[dim + 2 :])


def turned_blocks(parts, axes, order):
    inside = parts.shape[1:]
    filled = parts.reshape(*(lax.axis_size(a) for a in axes), *inside)
    for k in order:
        filled = lax.all_to_all(filled, axes[k], k, k, tiled=True)
    return filled.reshape(-1, *inside)


def exchange_by_chip(array, groups, order, split_dim, concat_dim):
    size = lax.axis_size(groups[0]) * lax.axis_size(groups[1])
    parts = cut_along(array, split_dim, size)
    return laid_out(turned_blocks(parts, groups, order), concat_dim)


def in_one_piece(arrays, axis, split_dim, concat_dim, along):
    widths = [a.shape[along] for a in arrays]
    both = jnp.concatenate(arrays, axis=along)
    filled = lax.all_to_all(both, axis, split_axis=split_dim, concat_axis=concat_dim, tiled=True)
    return tuple(jnp.split(filled, [sum(widths[:k]) for k in range(1, len(widths))], axis=along))


def copy_for_each(array, axis):
    copies = jnp.broadcast_to(array, (lax.axis_size(axis), *array.shape))
    return lax.all_to_all(copies, axis, split_axis=0, concat_axis=0, tiled=True)


def gather_directly(array, axis, dim):
    parts = copy_for_each(array, axis)
    return laid_out(parts, dim)


def dequantise(integer_levels, block_scales):
    shaped = integer_levels.astype(jnp.float32).reshape(block_scales.shape + (QBLOCK,))
    values = shaped * block_scales.astype(jnp.float32)[..., None]
    return values.reshape(integer_levels.shape)


def per_device(local_weights, base_weights, momentum):
    row_count, col_count = base_weights.shape
    replica_differences = base_weights - local_weights[0].astype(jnp.float32)
    block_grouped = replica_differences.reshape(row_count, col_count // QBLOCK, QBLOCK)
    block_scales = (jnp.max(jnp.abs(block_grouped), axis=2) + EPSILON).astype(jnp.bfloat16)
    integer_levels = (block_grouped / block_scales.astype(jnp.float32)[:, :, None]).astype(
        jnp.bfloat16
    )
    levels_local = integer_levels.reshape(1, row_count, col_count)
    scales_local = block_scales.reshape(1, row_count, col_count // QBLOCK)
    transmitted_levels, transmitted_scales = (
        exchange_by_chip(levels_local, (("fsdp_0", "fsdp_1"), "fsdp_2"), (1, 0), 2, 1),
        exchange_by_chip(scales_local, (("fsdp_0", "fsdp_1"), "fsdp_2"), (1, 0), 2, 1),
    )
    levels_owned, scales_owned = in_one_piece(
        (transmitted_levels, transmitted_scales), "replica", 1, 0, 2
    )
    summed = jnp.sum(dequantise(levels_owned, scales_owned), axis=0)
    average = summed / lax.axis_size("replica")
    new_momentum = MOMENTUM_COEF * momentum + average
    update = (LEARN_RATE * (average + MOMENTUM_COEF * new_momentum)).astype(jnp.bfloat16)
    gathered = gather_directly(update, "replica", 0)
    returned = lax.all_to_all(gathered, FSDP, split_axis=0, concat_axis=1, tiled=True)
    new_weights = base_weights - returned.astype(jnp.float32)
    return (new_weights, new_momentum)


def solution(mesh):
    finer = Mesh(
        mesh.devices.reshape(mesh.shape["replica"], 8, 2, 2),
        ("replica", "fsdp_0", "fsdp_1", "fsdp_2"),
    )
    in_specs = (P("replica", FSDP, None), P(FSDP, None), P("replica", FSDP))
    out_specs = (P(FSDP, None), P("replica", FSDP))
    return jax.shard_map(
        per_device, mesh=finer, in_specs=in_specs, out_specs=out_specs, check_vma=False
    )
```

profile of v0, /device:TPU:1, one launch (start us, length us, event | category | flops | bytes accessed | tf_op | source)
XLA Modules:
  0.0 261.5 jit_solution(4076040931034758202)
XLA Ops:
  0.6 4.9 %abs_bitcast_fusion = (f32[4,8,224,128]{3,1,2,0:T(8,128)S(1)}, f32[32,28672]{1,0:T(8,128)}) fusion(f32[32,28672]{1,0:T(8,128)} %param.4, bf16[1,32,28672]{2,1,0:T(8,128)(2,1)} %param.3), kind=kLoop, calls=%fused_computation.6 | loop fusion | flops 2752512 | bytes 12845056
  5.6 2.4 copy.55
  8.0 3.2 %reduce_max.9 = f32[32,224]{1,0:T(8,128)S(1)} reduce(f32[32,224,128]{2,1,0:T(8,128)} %bitcast.52, f32[]{:T(128)} %constant.1.clone.1), dimensions={2}, to_apply=%region_0.0 | reduce | flops 910336 | bytes 3698692 | tf_op jit(solution)/shard_map/reduce_max | solution.py:69
  11.4 0.7 reshape.79
  12.1 6.4 %all-to-all-start.2 = ((bf16[2,2,1792]{2,1,0:T(2,128)(2,1)}), bf16[2,2,1792]{2,1,0:T(2,128)(2,1)S(1)}, u32[]{:S(2)}, u32[]{:S(2)}) async-start(bf16[2,2,1792]{2,1,0:T(2,128)(2,1)} %reshape.79), calls=%async_computation.2 | async-start | bytes 28672 | tf_op jit(solution)/shard_map/all_to_all | solution.py:32
  18.5 2.3 div.23
  20.9 4.9 %div.24 = f32[1,32,32,896]{3,2,1,0:T(8,128)} reshape(f32[32,224,128]{2,1,0:T(8,128)} %div.23) | data formatting | bytes 7340032 | tf_op jit(solution)/shard_map/div | solution.py:70
  25.7 2.8 %copy.54 = f32[4,8,32,896]{3,2,1,0:T(8,128)S(1)} copy(f32[4,8,32,896]{3,1,2,0:T(8,128)} %bitcast.51) | data formatting | bytes 7340032
  28.6 0.3 copy-done
  28.9 1.9 fusion.2
  30.8 3.9 %reshape.74 = bf16[16,2,1,32,896]{4,1,0,3,2:T(2,128)(2,1)S(1)} reshape(bf16[32,1,32,896]{3,0,2,1:T(8,128)(2,1)} %fusion.2) | data formatting | bytes 3670016 | tf_op jit(solution)/shard_map/reshape | solution.py:30
  34.7 1.8 copy.30
  36.5 3.7 %all-to-all-start = ((bf16[16,2,1,32,896]{4,3,0,2,1:T(8,128)(2,1)}), bf16[16,2,1,32,896]{4,3,0,2,1:T(8,128)(2,1)S(1)}, u32[]{:S(2)}, u32[]{:S(2)}) async-start(bf16[16,2,1,32,896]{4,3,0,2,1:T(8,128)(2,1)} %copy.30), calls=%async_computation | async-start | bytes 3670016 | tf_op jit(solution)/shard_map/all_to_all | solution.py:32
  40.4 0.7 reshape.81
  41.1 1.4 all-to-all-done
  42.5 9.0 %all-to-all-start.3 = ((bf16[16,2,224]{2,1,0:T(2,128)(2,1)}), bf16[16,2,224]{2,1,0:T(2,128)(2,1)S(1)}, u32[]{:S(2)}, u32[]{:S(2)}) async-start(bf16[16,2,224]{2,1,0:T(2,128)(2,1)} %reshape.81), calls=%async_computation.3 | async-start | bytes 32768 | tf_op jit(solution)/shard_map/all_to_all | solution.py:32
  51.6 1.5 copy.31
  53.1 7.4 %all-to-all-done.3 = bf16[16,2,224]{2,1,0:T(2,128)(2,1)S(1)} async-done(((bf16[16,2,224]{2,1,0:T(2,128)(2,1)}), bf16[16,2,224]{2,1,0:T(2,128)(2,1)S(1)}, u32[]{:S(2)}, u32[]{:S(2)}) %all-to-all-start.3) | async-done | bytes 14368 | tf_op jit(solution)/shard_map/all_to_all | solution.py:32
  60.5 3.9 %all-to-all-start.1 = ((bf16[16,2,1,32,896]{4,3,1,2,0:T(8,128)(2,1)}), bf16[16,2,1,32,896]{4,3,1,2,0:T(8,128)(2,1)S(1)}, u32[]{:S(2)}, u32[]{:S(2)}) async-start(bf16[16,2,1,32,896]{4,3,1,2,0:T(8,128)(2,1)} %copy.31), calls=%async_computation.1 | async-start | bytes 3670016 | tf_op jit(solution)/shard_map/all_to_all | solution.py:32
  64.5 0.3 copy.46
  64.8 43.1 %all-to-all-done.1 = bf16[16,2,1,32,896]{4,3,1,2,0:T(8,128)(2,1)S(1)} async-done(((bf16[16,2,1,32,896]{4,3,1,2,0:T(8,128)(2,1)}), bf16[16,2,1,32,896]{4,3,1,2,0:T(8,128)(2,1)S(1)}, u32[]{:S(2)}, u32[]{:S(2)}) %all-to-all-start.1) | async-done | bytes 1835040 | tf_op jit(solution)/shard_map/all_to_all | solution.py:32
  107.9 0.3 pad_maximum_fusion
  108.2 5.2 %copy.62 = bf16[1,1024,903]{2,0,1:T(2,128)(2,1)} copy(bf16[1,1024,903]{2,1,0:T(8,128)(2,1)S(1)} %pad_maximum_fusion) | data formatting | bytes 3698688 | tf_op jit(solution)/shard_map/concatenate | solution.py:44
  113.4 0.5 broadcast.26
  113.9 13.2 %reduce = bf16[1024,903]{1,0:T(8,128)(2,1)S(1)} reduce(bf16[1024,1,903]{2,1,0:T(2,128)(2,1)} %bitcast.48, bf16[]{:T(256)} %broadcast.26), dimensions={1}, to_apply=%bitcast.44.reduce_sub_computation | reduce | bytes 3698690
  127.1 5.2 %reshape.83 = bf16[8,2,57792]{2,1,0:T(2,128)(2,1)} reshape(bf16[1024,903]{1,0:T(8,128)(2,1)S(1)} %reduce) | data formatting | bytes 3698688
  132.3 4.2 %all-to-all-start.4 = ((bf16[8,2,57792]{2,1,0:T(2,128)(2,1)}), bf16[8,2,57792]{2,1,0:T(2,128)(2,1)S(1)}, u32[]{:S(2)}, u32[]{:S(2)}) async-start(bf16[8,2,57792]{2,1,0:T(2,128)(2,1)} %reshape.83), calls=%async_computation.4 | async-start | bytes 3702784 | tf_op jit(solution)/shard_map/all_to_all | solution.py:45
  136.5 0.2 copy.42
  136.7 20.1 %all-to-all-done.4 = bf16[8,2,57792]{2,1,0:T(2,128)(2,1)S(1)} async-done(((bf16[8,2,57792]{2,1,0:T(2,128)(2,1)}), bf16[8,2,57792]{2,1,0:T(2,128)(2,1)S(1)}, u32[]{:S(2)}, u32[]{:S(2)}) %all-to-all-start.4) | async-done | bytes 1849376 | tf_op jit(solution)/shard_map/all_to_all | solution.py:45
  156.8 5.0 %reshape.84 = bf16[1024,1,903]{2,1,0:T(2,128)(2,1)} reshape(bf16[8,2,57792]{2,1,0:T(2,128)(2,1)S(1)} %all-to-all-done.4) | data formatting | bytes 3698688
  161.8 3.0 %copy.49 = bf16[1,1024,903]{2,1,0:T(8,128)(2,1)S(1)} copy(bf16[1,1024,903]{2,0,1:T(2,128)(2,1)} %bitcast.49) | data formatting | bytes 3698688
  164.8 0.2 split.8
  165.0 0.1 copy.52
  165.2 2.7 %copy.51 = bf16[8,128,896]{1,0,2:T(8,128)(2,1)} copy(bf16[8,128,896]{2,1,0:T(8,128)(2,1)S(1)} %split.8) | data formatting | bytes 3670016
  167.9 0.2 mul.23
  168.2 1.3 copy-done.2
  169.4 3.1 %fusion.1 = f32[128,896]{0,1:T(8,128)S(1)} fusion(f32[8,128,896]{1,2,0:T(8,128)S(1)} %bitcast.53, bf16[8,128,896]{1,0,2:T(8,128)(2,1)S(1)} %copy-done.2), kind=kLoop, calls=%fused_computation.4 | loop fusion | flops 2637824 | bytes 5963776 | tf_op jit(solution)/shard_map/reduce_sum | solution.py:82
  172.5 0.1 multiply_add_fusion
  172.7 0.2 copy.43
  172.8 0.2 broadcast_in_dim.2
  173.1 25.6 %all_to_all.50 = bf16[8,128,896]{2,1,0:T(8,128)(2,1)} all-to-all(bf16[8,128,896]{2,1,0:T(8,128)(2,1)S(1)} %broadcast_in_dim.2), channel_id=1, replica_groups=mesh['replica'=8,'fsdp_0'=8,'fsdp_1'=2,'fsdp_2'=2] {'replica'}, dimensions={0} | all-to-all | bytes 3670016 | tf_op jit(solution)/shard_map/all_to_all | solution.py:51
  198.6 13.5 %all-to-all-start.6 = ((bf16[32,32,896]{2,1,0:T(8,128)(2,1)}), bf16[32,32,896]{2,1,0:T(8,128)(2,1)S(1)}, u32[]{:S(2)}, u32[]{:S(2)}) async-start(bf16[32,32,896]{2,1,0:T(8,128)(2,1)} %bitcast.7), calls=%async_computation.6 | async-start | bytes 3670016 | tf_op jit(solution)/shard_map/all_to_all | solution.py:87
  212.2 1.0 copy.45
  213.1 43.6 %all-to-all-done.6 = bf16[32,32,896]{2,1,0:T(8,128)(2,1)S(1)} async-done(((bf16[32,32,896]{2,1,0:T(8,128)(2,1)}), bf16[32,32,896]{2,1,0:T(8,128)(2,1)S(1)}, u32[]{:S(2)}, u32[]{:S(2)}) %all-to-all-start.6) | async-done | bytes 1835040 | tf_op jit(solution)/shard_map/all_to_all | solution.py:87
  256.8 0.5 convert_bitcast_fusion
  257.3 0.2 copy.53
  257.5 1.8 copy-done.1
  259.3 2.2 sub.7
  (15 shorter events, 0.5 us)
Async XLA Ops:
  12.1 24.4 %all-to-all-start.2 = ((bf16[2,2,1792]{2,1,0:T(2,128)(2,1)}), bf16[2,2,1792]{2,1,0:T(2,128)(2,1)S(1)}, u32[]{:S(2)}, u32[]{:S(2)}) async-start(bf16[2,2,1792]{2,1,0:T(2,128)(2,1)} %reshape.79), calls=%async_computation.2 | async-start | bytes 28672 | tf_op jit(solution)/shard_map/all_to_all | solution.py:32
  25.7 3.1 %copy-start = (f32[1,32,32,896]{3,2,1,0:T(8,128)S(1)}, f32[1,32,32,896]{3,2,1,0:T(8,128)}, u32[]{:S(2)}) copy-start(f32[1,32,32,896]{3,2,1,0:T(8,128)} %div.24) | copy-start | bytes 11010052
  36.5 6.1 %all-to-all-start = ((bf16[16,2,1,32,896]{4,3,0,2,1:T(8,128)(2,1)}), bf16[16,2,1,32,896]{4,3,0,2,1:T(8,128)(2,1)S(1)}, u32[]{:S(2)}, u32[]{:S(2)}) async-start(bf16[16,2,1,32,896]{4,3,0,2,1:T(8,128)(2,1)} %copy.30), calls=%async_computation | async-start | bytes 3670016 | tf_op jit(solution)/shard_map/all_to_all | solution.py:32
  42.5 18.0 %all-to-all-start.3 = ((bf16[16,2,224]{2,1,0:T(2,128)(2,1)}), bf16[16,2,224]{2,1,0:T(2,128)(2,1)S(1)}, u32[]{:S(2)}, u32[]{:S(2)}) async-start(bf16[16,2,224]{2,1,0:T(2,128)(2,1)} %reshape.81), calls=%async_computation.3 | async-start | bytes 32768 | tf_op jit(solution)/shard_map/all_to_all | solution.py:32
  60.5 47.4 %all-to-all-start.1 = ((bf16[16,2,1,32,896]{4,3,1,2,0:T(8,128)(2,1)}), bf16[16,2,1,32,896]{4,3,1,2,0:T(8,128)(2,1)S(1)}, u32[]{:S(2)}, u32[]{:S(2)}) async-start(bf16[16,2,1,32,896]{4,3,1,2,0:T(8,128)(2,1)} %copy.31), calls=%async_computation.1 | async-start | bytes 3670016 | tf_op jit(solution)/shard_map/all_to_all | solution.py:32
  127.1 9.4 %copy-start.3 = (f32[128,896]{1,0:T(8,128)S(1)}, f32[128,896]{1,0:T(8,128)}, u32[]{:S(2)}) copy-start(f32[128,896]{1,0:T(8,128)} %param.5) | copy-start | bytes 1376260
  132.3 24.5 %all-to-all-start.4 = ((bf16[8,2,57792]{2,1,0:T(2,128)(2,1)}), bf16[8,2,57792]{2,1,0:T(2,128)(2,1)S(1)}, u32[]{:S(2)}, u32[]{:S(2)}) async-start(bf16[8,2,57792]{2,1,0:T(2,128)(2,1)} %reshape.83), calls=%async_computation.4 | async-start | bytes 3702784 | tf_op jit(solution)/shard_map/all_to_all | solution.py:45
  167.9 1.5 copy-start.2
  198.6 58.1 %all-to-all-start.6 = ((bf16[32,32,896]{2,1,0:T(8,128)(2,1)}), bf16[32,32,896]{2,1,0:T(8,128)(2,1)S(1)}, u32[]{:S(2)}, u32[]{:S(2)}) async-start(bf16[32,32,896]{2,1,0:T(8,128)(2,1)} %bitcast.7), calls=%async_computation.6 | async-start | bytes 3670016 | tf_op jit(solution)/shard_map/all_to_all | solution.py:87
  257.2 2.0 copy-start.1
where the time goes:
time: 262 us; the launch traced here: 261 us
  waiting for transfers between devices  116 us (44%)
  local copies, waits for them, and re-layouts  49.2 us (19%)
  starting transfers between devices  40.8 us (16%)
  other arithmetic  29.4 us (11%)
  blocking collectives  25.6 us (10%)
    all_to_all x4, waiting for transfers between devices, turned_blocks(): filled = lax.all_to_all(filled, axes[k], k, k, tiled=True)  52 us
    all_to_all x1, waiting for transfers between devices, per_device(): lax.all_to_all(gathered, FSDP, split_axis=0, concat_axis=1, tiled=True)  43.6 us
    unnamed x22, local copies, waits for them, and re-layouts  27.9 us
    all_to_all x1, blocking collectives, copy_for_each(): return lax.all_to_all(copies, axis, split_axis=0, concat_axis=0, tiled=True)  25.6 us
    all_to_all x4, starting transfers between devices, turned_blocks(): filled = lax.all_to_all(filled, axes[k], k, k, tiled=True)  23.1 us
    all_to_all x1, waiting for transfers between devices, in_one_piece(): lax.all_to_all(both, axis, split_axis=split_dim, concat_axis=concat_dim,...  20.1 us
    unnamed x3, other arithmetic  18.6 us
    all_to_all x1, starting transfers between devices, per_device(): lax.all_to_all(gathered, FSDP, split_axis=0, concat_axis=1, tiled=True)  13.5 us
  transfers between devices with their start and end apart: 6, of which 5 were waited for; matrix products, arithmetic and copies ran while one was open for 8% of the time, Pallas kernels for 0%

commit v1 on v0

v1 whole, which is shorter than its diff:
```python
import jax
import jax.numpy as jnp
from jax import lax
from jax.experimental import pallas as pl
from jax.experimental.pallas import tpu as pltpu
from jax.sharding import Mesh
from jax.sharding import PartitionSpec as P

R = ("y", "xl")
J = ("xh", "c")
FSDP = ("z", "xh", "c")
LEARN_RATE = 0.7
MOMENTUM_COEF = 0.9
CHUNKS = 2


def delta_parts(local, base, z, chunk, width):
    rows = base.shape[0]
    count = local.shape[1] // (CHUNKS * width)

    def body(z_ref, local_ref, base_ref, out_ref):
        out_ref[...] = (base_ref[...] - local_ref[...].astype(jnp.float32)).astype(jnp.bfloat16)

    def block(r, z_ref):
        return (0, CHUNKS * (r ^ z_ref[0]) + chunk)

    return pl.pallas_call(
        body,
        grid_spec=pltpu.PrefetchScalarGridSpec(
            num_scalar_prefetch=1,
            grid=(count,),
            in_specs=[pl.BlockSpec((rows, width), block), pl.BlockSpec((rows, width), block)],
            out_specs=pl.BlockSpec((None, rows, width), lambda r, z_ref: (r, 0, 0)),
        ),
        out_shape=jax.ShapeDtypeStruct((count, rows, width), jnp.bfloat16),
        name=f"delta_{chunk}",
    )(z, local, base)


def sum_update(parts, momentum, chunk):
    count, rows, width = parts.shape
    pieces, _, inner = momentum.shape
    mine = pieces // CHUNKS

    def body(parts_ref, m_ref, out_ref, avg_ref):
        for p in range(mine):
            for k in range(0, inner, 128):
                col = p * inner + k
                total = parts_ref[0, :, col : col + 128].astype(jnp.float32)
                for r in range(1, count):
                    total = total + parts_ref[r, :, col : col + 128].astype(jnp.float32)
                average = total * (1.0 / count)
                old = m_ref[chunk * mine + p, :, k : k + 128].astype(jnp.float32)
                new = MOMENTUM_COEF * old + average
                update = (LEARN_RATE * (average + MOMENTUM_COEF * new)).astype(jnp.bfloat16)
                avg_ref[p, :, k : k + 128] = average.astype(jnp.bfloat16)
                for r in range(count):
                    out_ref[r, :, col : col + 128] = update

    return pl.pallas_call(
        body,
        in_specs=[pl.BlockSpec(memory_space=pltpu.VMEM)] * 2,
        out_specs=[pl.BlockSpec(memory_space=pltpu.VMEM)] * 2,
        out_shape=[
            jax.ShapeDtypeStruct(parts.shape, jnp.bfloat16),
            jax.ShapeDtypeStruct((mine, rows, inner), jnp.bfloat16),
        ],
        name=f"update_{chunk}",
    )(parts, momentum)


def apply_update(base, parts, z, chunk, earlier):
    count, rows, width = parts.shape

    def body(z_ref, base_ref, part_ref, *refs):
        refs[-1][...] = base_ref[...] - part_ref[...].astype(jnp.float32)

    def block(r, z_ref):
        return (0, CHUNKS * (r ^ z_ref[0]) + chunk)

    more = [] if earlier is None else [earlier]
    return pl.pallas_call(
        body,
        grid_spec=pltpu.PrefetchScalarGridSpec(
            num_scalar_prefetch=1,
            grid=(count,),
            in_specs=[
                pl.BlockSpec((rows, width), block),
                pl.BlockSpec((None, rows, width), lambda r, z_ref: (r, 0, 0)),
            ]
            + [pl.BlockSpec(memory_space=pl.ANY)] * len(more),
            out_specs=pl.BlockSpec((rows, width), block),
        ),
        out_shape=jax.ShapeDtypeStruct(base.shape, base.dtype),
        input_output_aliases={3: 0} if more else {},
        name=f"apply_{chunk}",
    )(z, base, parts, *more)


def per_device(local_weights, base_weights, momentum):
    count = lax.axis_size(R)
    rows, cols = base_weights.shape
    width = cols // (count * CHUNKS)
    z = lax.axis_index("z").reshape(1)
    local = local_weights[0]
    there = [(r * count + p, (r ^ p) * count + r) for r in range(count) for p in range(count)]
    back = [(b, a) for a, b in there]
    pieces = lax.axis_size(J)

    summed = []
    for c in range(CHUNKS):
        parts = delta_parts(local, base_weights, z, c, width)
        summed.append(lax.all_to_all(parts, R, 0, 0, tiled=True))
        if c == 0:
            m = momentum.astype(jnp.bfloat16).reshape(pieces, rows, -1)
            m = lax.all_to_all(m, J, 0, 0, tiled=True)
            m = lax.ppermute(m, R + ("z",), there)
    averages, updates = [], []
    for c in range(CHUNKS):
        copies, average = sum_update(summed[c], m, c)
        averages.append(average)
        updates.append(lax.all_to_all(copies, R, 0, 0, tiled=True))
    average = lax.ppermute(jnp.concatenate(averages), R + ("z",), back)
    average = lax.all_to_all(average, J, 0, 0, tiled=True)
    new_momentum = MOMENTUM_COEF * momentum + average.reshape(momentum.shape).astype(jnp.float32)
    new_weights = None
    for c in range(CHUNKS):
        new_weights = apply_update(base_weights, updates[c], z, c, new_weights)
    return new_weights, new_momentum


def solution(mesh):
    finer = Mesh(mesh.devices.reshape(4, 2, 8, 2, 2), ("y", "xl", "z", "xh", "c"))
    in_specs = (P(R, FSDP, None), P(FSDP, None), P(R, FSDP))
    out_specs = (P(FSDP, None), P(R, FSDP))
    return jax.shard_map(per_device, mesh=finer, in_specs=in_specs, out_specs=out_specs, check_vma=False)
```

time: 262 us -> 146 us (0.56)
  the two profiles are of different devices: /device:TPU:1 before, /device:TPU:160 now
where the time goes in v1:
time: 146 us; the launch traced here: 145 us
  waiting for transfers between devices  58.1 us (40%)
  blocking collectives  30.4 us (21%)
  Pallas kernels  27.8 us (19%)
  starting transfers between devices  22 us (15%)
  other arithmetic  3.55 us (2%)
  local copies, waits for them, and re-layouts  2.54 us (2%)
    ppermute x1, waiting for transfers between devices, per_device(): m = lax.ppermute(m, R + ('z',), there)  29.2 us
    all_to_all x1, blocking collectives, per_device(): updates.append(lax.all_to_all(copies, R, 0, 0, tiled=True))  18.7 us
    ppermute x1, waiting for transfers between devices, per_device(): average = lax.ppermute(jnp.concatenate(averages), R + ('z',), back)  12.3 us
    pallas_call x2, Pallas kernels, apply_update(): pl.pallas_call(body, grid_spec=pltpu.PrefetchScalarGridSpec(num_scalar_pr...  11.7 us
    all_to_all x1, blocking collectives, per_device(): average = lax.all_to_all(average, J, 0, 0, tiled=True)  11.7 us
    pallas_call x2, Pallas kernels, delta_parts(): pl.pallas_call(body, grid_spec=pltpu.PrefetchScalarGridSpec(num_scalar_pr...  11.3 us
    all_to_all x2, waiting for transfers between devices, per_device(): summed.append(lax.all_to_all(parts, R, 0, 0, tiled=True))  8.36 us
    all_to_all x2, starting transfers between devices, per_device(): summed.append(lax.all_to_all(parts, R, 0, 0, tiled=True))  8.05 us
  transfers between devices with their start and end apart: 6, of which 5 were waited for; matrix products, arithmetic and copies ran while one was open for 1% of the time, Pallas kernels for 13%

profile of v1, /device:TPU:160, one launch (start us, length us, event | category | flops | bytes accessed | tf_op | source)
XLA Modules:
  0.0 145.0 jit_solution(3096507888918743619)
XLA Ops:
  0.6 1.7 %convert_element_type.9 = bf16[128,896]{1,0:T(8,128)(2,1)} convert(f32[128,896]{1,0:T(8,128)} %param.5) | non-fusion elementwise | flops 114688 | bytes 688128 | tf_op jit(solution)/shard_map/convert_element_type | solution.py:115
  2.4 4.3 %all-to-all-start.1 = ((bf16[4,32,896]{2,1,0:T(8,128)(2,1)}), bf16[4,32,896]{2,1,0:T(8,128)(2,1)S(1)}, u32[]{:S(2)}, u32[]{:S(2)}) async-start(bf16[4,32,896]{2,1,0:T(8,128)(2,1)} %bitcast.2), calls=%async_computation.1 | async-start | bytes 458752 | tf_op jit(solution)/shard_map/all_to_all | solution.py:116
  6.7 5.6 %delta_0.1 = bf16[8,32,1792]{2,1,0:T(8,128)(2,1)} custom-call(s32[1]{0:T(128)} %bitcast.z_ref, bf16[32,28672]{1,0:T(8,128)(2,1)} %bitcast.6, f32[32,28672]{1,0:T(8,128)} %base_ref.7), custom_call_target="tpu_custom_call" | custom-call | tf_op jit(solution)/shard_map/delta_0/pallas_call | solution.py:27
  12.3 1.5 %all-to-all-done.1 = bf16[4,32,896]{2,1,0:T(8,128)(2,1)S(1)} async-done(((bf16[4,32,896]{2,1,0:T(8,128)(2,1)}), bf16[4,32,896]{2,1,0:T(8,128)(2,1)S(1)}, u32[]{:S(2)}, u32[]{:S(2)}) %all-to-all-start.1) | async-done | bytes 229408 | tf_op jit(solution)/shard_map/all_to_all | solution.py:116
  13.8 4.5 %all-to-all-start.3 = ((bf16[8,32,1792]{2,1,0:T(8,128)(2,1)}), bf16[8,32,1792]{2,1,0:T(8,128)(2,1)S(1)}, u32[]{:S(2)}, u32[]{:S(2)}) async-start(bf16[8,32,1792]{2,1,0:T(8,128)(2,1)} %delta_0.1), calls=%async_computation.3 | async-start | bytes 1835008 | tf_op jit(solution)/shard_map/all_to_all | solution.py:113
  18.3 5.6 %delta_1.1 = bf16[8,32,1792]{2,1,0:T(8,128)(2,1)} custom-call(s32[1]{0:T(128)} %bitcast.z_ref, bf16[32,28672]{1,0:T(8,128)(2,1)} %bitcast.7, f32[32,28672]{1,0:T(8,128)} %base_ref.7), custom_call_target="tpu_custom_call" | custom-call | tf_op jit(solution)/shard_map/delta_1/pallas_call | solution.py:27
  24.0 8.4 %all-to-all-done.3.parts_ref = bf16[8,32,1792]{2,1,0:T(8,128)(2,1)S(1)} async-done(((bf16[8,32,1792]{2,1,0:T(8,128)(2,1)}), bf16[8,32,1792]{2,1,0:T(8,128)(2,1)S(1)}, u32[]{:S(2)}, u32[]{:S(2)}) %all-to-all-start.3) | async-done | bytes 917536 | tf_op jit(solution)/shard_map/all_to_all | solution.py:113
  32.3 0.0 copy-start.1
  32.3 3.6 %all-to-all-start = ((bf16[8,32,1792]{2,1,0:T(8,128)(2,1)}), bf16[8,32,1792]{2,1,0:T(8,128)(2,1)S(1)}, u32[]{:S(2)}, u32[]{:S(2)}) async-start(bf16[8,32,1792]{2,1,0:T(8,128)(2,1)} %delta_1.1), calls=%async_computation | async-start | bytes 1835008 | tf_op jit(solution)/shard_map/all_to_all | solution.py:113
  35.9 0.0 copy-start.3
  35.9 4.1 %collective-permute-start = (bf16[4,32,896]{2,1,0:T(8,128)(2,1)S(1)}, bf16[4,32,896]{2,1,0:T(8,128)(2,1)S(1)}, u32[]{:S(2)}, u32[]{:S(2)}) collective-permute-start(bf16[4,32,896]{2,1,0:T(8,128)(2,1)S(1)} %all-to-all-done.1), channel_id=1, source_target_pairs={{0,0},{4,32},{8,64},{12,96},{16,128},{20,160},{24,192},{28,224},{3... | collective-permute-start | bytes 688136 | tf_op jit(solution)/shard_map/ppermute | solution.py:117
  40.0 29.2 %collective-permute-done.m_ref = bf16[4,32,896]{2,1,0:T(8,128)(2,1)S(1)} collective-permute-done((bf16[4,32,896]{2,1,0:T(8,128)(2,1)S(1)}, bf16[4,32,896]{2,1,0:T(8,128)(2,1)S(1)}, u32[]{:S(2)}, u32[]{:S(2)}) %collective-permute-start) | collective-permute-done | bytes 229408 | tf_op jit(solution)/shard_map/ppermute | solution.py:117
  69.3 0.0 copy-done.1
  69.3 0.0 copy-start.4
  69.3 0.7 copy-done.4
  70.0 2.4 %update_0.1 = (bf16[8,32,1792]{2,1,0:T(8,128)(2,1)}, bf16[2,32,896]{2,1,0:T(8,128)(2,1)}) custom-call(bf16[8,32,1792]{2,1,0:T(8,128)(2,1)} %copy-done.1, bf16[4,32,896]{2,1,0:T(8,128)(2,1)} %copy-done.4), custom_call_target="tpu_custom_call" | custom-call | tf_op jit(solution)/shard_map/update_0/pallas_call | solution.py:60
  72.3 0.0 all-to-all-done.parts_ref
  72.3 0.0 copy-start.2
  72.3 0.9 copy-done.2
  73.2 2.4 %update_1.1 = (bf16[8,32,1792]{2,1,0:T(8,128)(2,1)}, bf16[2,32,896]{2,1,0:T(8,128)(2,1)}) custom-call(bf16[8,32,1792]{2,1,0:T(8,128)(2,1)} %copy-done.2, bf16[4,32,896]{2,1,0:T(8,128)(2,1)} %copy-done.4), custom_call_target="tpu_custom_call" | custom-call | tf_op jit(solution)/shard_map/update_1/pallas_call | solution.py:60
  75.7 1.0 pad_maximum_fusion
  76.7 1.9 %collective-permute-start.1 = (bf16[4,32,896]{2,1,0:T(8,128)(2,1)S(1)}, bf16[4,32,896]{2,1,0:T(8,128)(2,1)S(1)}, u32[]{:S(2)}, u32[]{:S(2)}) collective-permute-start(bf16[4,32,896]{2,1,0:T(8,128)(2,1)S(1)} %pad_maximum_fusion), channel_id=1, source_target_pairs={{0,0},{32,4},{64,8},{96,12},{128,16},{160,20},{192,24},{224,28},{3... | collective-permute-start | bytes 688136 | tf_op jit(solution)/shard_map/ppermute | solution.py:123
  78.6 12.3 %collective-permute-done.1 = bf16[4,32,896]{2,1,0:T(8,128)(2,1)S(1)} collective-permute-done((bf16[4,32,896]{2,1,0:T(8,128)(2,1)S(1)}, bf16[4,32,896]{2,1,0:T(8,128)(2,1)S(1)}, u32[]{:S(2)}, u32[]{:S(2)}) %collective-permute-start.1) | collective-permute-done | bytes 229408 | tf_op jit(solution)/shard_map/ppermute | solution.py:123
  90.9 11.7 %all_to_all.30 = bf16[4,32,896]{2,1,0:T(8,128)(2,1)S(1)} all-to-all(bf16[4,32,896]{2,1,0:T(8,128)(2,1)S(1)} %collective-permute-done.1), channel_id=1, replica_groups=mesh['y'=4,'xl'=2,'z'=8,'xh'=2,'c'=2] {'xh','c'}, dimensions={0} | all-to-all | bytes 458752 | tf_op jit(solution)/shard_map/all_to_all | solution.py:124
  102.6 18.7 %all_to_all.31.part_ref = bf16[8,32,1792]{2,1,0:T(8,128)(2,1)} all-to-all(bf16[8,32,1792]{2,1,0:T(8,128)(2,1)} %get-tuple-element.7), channel_id=1, replica_groups=mesh['y'=4,'xl'=2,'z'=8,'xh'=2,'c'=2] {'y','xl'}, dimensions={0} | all-to-all | bytes 1835008 | tf_op jit(solution)/shard_map/all_to_all | solution.py:122
  121.3 3.6 %all-to-all-start.2 = ((bf16[8,32,1792]{2,1,0:T(8,128)(2,1)}), bf16[8,32,1792]{2,1,0:T(8,128)(2,1)S(1)}, u32[]{:S(2)}, u32[]{:S(2)}) async-start(bf16[8,32,1792]{2,1,0:T(8,128)(2,1)} %get-tuple-element.6), calls=%async_computation.2 | async-start | bytes 1835008 | tf_op jit(solution)/shard_map/all_to_all | solution.py:122
  124.8 0.0 copy-done.3
  124.8 0.8 convert_add_fusion
  125.7 5.9 %apply_0.1.refs_0_ = f32[32,28672]{1,0:T(8,128)} custom-call(s32[1]{0:T(128)} %bitcast.z_ref, f32[32,28672]{1,0:T(8,128)} %base_ref.7, bf16[8,32,1792]{2,1,0:T(8,128)(2,1)} %all_to_all.31.part_ref), custom_call_target="tpu_custom_call" | custom-call | tf_op jit(solution)/shard_map/apply_0/pallas_call | solution.py:82
  131.5 6.7 %all-to-all-done.2.part_ref = bf16[8,32,1792]{2,1,0:T(8,128)(2,1)S(1)} async-done(((bf16[8,32,1792]{2,1,0:T(8,128)(2,1)}), bf16[8,32,1792]{2,1,0:T(8,128)(2,1)S(1)}, u32[]{:S(2)}, u32[]{:S(2)}) %all-to-all-start.2) | async-done | bytes 917536 | tf_op jit(solution)/shard_map/all_to_all | solution.py:122
  138.2 0.0 copy-start
  138.2 0.9 copy-done
  139.2 5.9 %apply_1.1 = f32[32,28672]{1,0:T(8,128)} custom-call(s32[1]{0:T(128)} %bitcast.z_ref, f32[32,28672]{1,0:T(8,128)} %base_ref.7, bf16[8,32,1792]{2,1,0:T(8,128)(2,1)} %copy-done, f32[32,28672]{1,0:T(8,128)} %apply_0.1.refs_0_), custom_call_target="tpu_custom_call", output_to_operand_aliasing={{}: (3, {})} | custom-call | tf_op jit(solution)/shard_map/apply_1/pallas_call | solution.py:82
Async XLA Ops:
  2.4 11.5 %all-to-all-start.1 = ((bf16[4,32,896]{2,1,0:T(8,128)(2,1)}), bf16[4,32,896]{2,1,0:T(8,128)(2,1)S(1)}, u32[]{:S(2)}, u32[]{:S(2)}) async-start(bf16[4,32,896]{2,1,0:T(8,128)(2,1)} %bitcast.2), calls=%async_computation.1 | async-start | bytes 458752 | tf_op jit(solution)/shard_map/all_to_all | solution.py:116
  13.8 18.5 %all-to-all-start.3 = ((bf16[8,32,1792]{2,1,0:T(8,128)(2,1)}), bf16[8,32,1792]{2,1,0:T(8,128)(2,1)S(1)}, u32[]{:S(2)}, u32[]{:S(2)}) async-start(bf16[8,32,1792]{2,1,0:T(8,128)(2,1)} %delta_0.1), calls=%async_computation.3 | async-start | bytes 1835008 | tf_op jit(solution)/shard_map/all_to_all | solution.py:113
  32.3 37.0 %copy-start.1 = (bf16[8,32,1792]{2,1,0:T(8,128)(2,1)}, bf16[8,32,1792]{2,1,0:T(8,128)(2,1)S(1)}, u32[]{:S(2)}) copy-start(bf16[8,32,1792]{2,1,0:T(8,128)(2,1)S(1)} %all-to-all-done.3.parts_ref) | copy-start | bytes 2752516
  32.3 40.0 %all-to-all-start = ((bf16[8,32,1792]{2,1,0:T(8,128)(2,1)}), bf16[8,32,1792]{2,1,0:T(8,128)(2,1)S(1)}, u32[]{:S(2)}, u32[]{:S(2)}) async-start(bf16[8,32,1792]{2,1,0:T(8,128)(2,1)} %delta_1.1), calls=%async_computation | async-start | bytes 1835008 | tf_op jit(solution)/shard_map/all_to_all | solution.py:113
  35.9 88.9 %copy-start.3 = (f32[128,896]{1,0:T(8,128)S(1)}, f32[128,896]{1,0:T(8,128)}, u32[]{:S(2)}) copy-start(f32[128,896]{1,0:T(8,128)} %param.5) | copy-start | bytes 1376260
  35.9 33.4 %collective-permute-start = (bf16[4,32,896]{2,1,0:T(8,128)(2,1)S(1)}, bf16[4,32,896]{2,1,0:T(8,128)(2,1)S(1)}, u32[]{:S(2)}, u32[]{:S(2)}) collective-permute-start(bf16[4,32,896]{2,1,0:T(8,128)(2,1)S(1)} %all-to-all-done.1), channel_id=1, source_target_pairs={{0,0},{4,32},{8,64},{12,96},{16,128},{20,160},{24,192},{28,224},{3... | collective-permute-start | bytes 688136 | tf_op jit(solution)/shard_map/ppermute | solution.py:117
  69.3 0.7 copy-start.4
  72.3 0.9 copy-start.2
  76.7 14.2 %collective-permute-start.1 = (bf16[4,32,896]{2,1,0:T(8,128)(2,1)S(1)}, bf16[4,32,896]{2,1,0:T(8,128)(2,1)S(1)}, u32[]{:S(2)}, u32[]{:S(2)}) collective-permute-start(bf16[4,32,896]{2,1,0:T(8,128)(2,1)S(1)} %pad_maximum_fusion), channel_id=1, source_target_pairs={{0,0},{32,4},{64,8},{96,12},{128,16},{160,20},{192,24},{224,28},{3... | collective-permute-start | bytes 688136 | tf_op jit(solution)/shard_map/ppermute | solution.py:123
  121.3 17.0 %all-to-all-start.2 = ((bf16[8,32,1792]{2,1,0:T(8,128)(2,1)}), bf16[8,32,1792]{2,1,0:T(8,128)(2,1)S(1)}, u32[]{:S(2)}, u32[]{:S(2)}) async-start(bf16[8,32,1792]{2,1,0:T(8,128)(2,1)} %get-tuple-element.6), calls=%async_computation.2 | async-start | bytes 1835008 | tf_op jit(solution)/shard_map/all_to_all | solution.py:122
  138.2 0.9 copy-start

commit v2 on v0

v2 whole, which is shorter than its diff:
```python
import jax
import jax.numpy as jnp
import numpy as np
from jax import lax
from jax.experimental import pallas as pl
from jax.experimental.pallas import tpu as pltpu
from jax.sharding import Mesh
from jax.sharding import PartitionSpec as P

R = ("y", "xl")
FSDP = ("z", "xh", "c")
EVERY = R + FSDP
LEARN_RATE = 0.7
MOMENTUM_COEF = 0.9
HALF = 16
WIDE = 896

MASKS = {"x": 1, "a": 2, "b": 6}
PARTS = (("xab", (0, 1, 2)), ("abx", (3, 4, 5)), ("bxa", (6, 7)))


def column_plane(r, z, c):
    return r ^ z ^ (7 * c)


def device(r, z, xh, c):
    return ((r * 8 + z) * 2 + xh) * 2 + c


def pairs(there):
    found = []
    for r in range(8):
        for z in range(8):
            for xh in range(2):
                for c in range(2):
                    found.append((device(r, z, xh, c), device(*there(r, z, xh, c))))
    return found


def send(value, there):
    return lax.ppermute(value, EVERY, pairs(there))


def exchange(value, dim):
    return send(value, lambda r, z, xh, c: (r ^ MASKS[dim], z, xh, c))


def peer(order, first, second, third):
    return (first * MASKS[order[0]]) ^ (second * MASKS[order[1]]) ^ (third * MASKS[order[2]])


def blocks_of(half):
    listed = []
    for p, (order, units) in enumerate(PARTS):
        for second in range(2):
            for third in range(2):
                for n, unit in enumerate(units):
                    listed.append((p, (second * 2 + third, n), peer(order, half, second, third), unit))
    return listed


def place_of(peer_index, unit):
    r = lax.axis_index(R) ^ peer_index
    z, xh, c = lax.axis_index("z"), lax.axis_index("xh"), lax.axis_index("c")
    core = c ^ (unit // 4)
    column = 4 * column_plane(r, z, core) + 2 * (xh ^ (unit // 2 % 2)) + core
    return HALF * (unit % 2), pl.multiple_of(column * WIDE, 128)


def shapes_of():
    return [(4, len(units), HALF, WIDE) for _, units in PARTS]


def deltas(local, base, half):
    blocks = blocks_of(half)

    def body(local_hbm, base_hbm, *refs):
        outs, (local_buf, base_buf, local_sem, base_sem) = refs[:3], refs[3:]
        copies = []
        for n, (_, _, k, unit) in enumerate(blocks):
            row, col = place_of(k, unit)
            here = (pl.ds(row, HALF), pl.ds(col, WIDE))
            one = pltpu.make_async_copy(base_hbm.at[here], base_buf.at[n], base_sem.at[n])
            two = pltpu.make_async_copy(local_hbm.at[here], local_buf.at[n], local_sem.at[n])
            one.start()
            two.start()
            copies.append((one, two))
        for n, (p, at, _, _) in enumerate(blocks):
            for copy in copies[n]:
                copy.wait()
            outs[p][at] = (base_buf[n] - local_buf[n].astype(jnp.float32)).astype(jnp.bfloat16)

    return pl.pallas_call(
        body,
        in_specs=[pl.BlockSpec(memory_space=pl.ANY)] * 2,
        out_specs=[pl.BlockSpec(memory_space=pltpu.VMEM)] * 3,
        out_shape=[jax.ShapeDtypeStruct(s, jnp.bfloat16) for s in shapes_of()],
        scratch_shapes=[
            pltpu.VMEM((len(blocks), HALF, WIDE), jnp.bfloat16),
            pltpu.VMEM((len(blocks), HALF, WIDE), jnp.float32),
            pltpu.SemaphoreType.DMA((len(blocks),)),
            pltpu.SemaphoreType.DMA((len(blocks),)),
        ],
        name=f"delta_{half}",
    )(local, base)


def apply_updates(base, updates, half, earlier):
    blocks = blocks_of(half)

    def body(base_hbm, *refs):
        parts, out_hbm = refs[:3], refs[-5]
        base_buf, out_buf, base_sem, out_sem = refs[-4:]
        copies = []
        for n, (_, _, k, unit) in enumerate(blocks):
            row, col = place_of(k, unit)
            here = (pl.ds(row, HALF), pl.ds(col, WIDE))
            one = pltpu.make_async_copy(base_hbm.at[here], base_buf.at[n], base_sem.at[n])
            two = pltpu.make_async_copy(out_buf.at[n], out_hbm.at[here], out_sem.at[n])
            one.start()
            copies.append((one, two))
        for n, (p, at, _, _) in enumerate(blocks):
            copies[n][0].wait()
            out_buf[n] = base_buf[n] - parts[p][at].astype(jnp.float32)
            copies[n][1].start()
        for n in range(len(blocks)):
            copies[n][1].wait()

    more = [] if earlier is None else [earlier]
    return pl.pallas_call(
        body,
        in_specs=[pl.BlockSpec(memory_space=pl.ANY)]
        + [pl.BlockSpec(memory_space=pltpu.VMEM)] * 3
        + [pl.BlockSpec(memory_space=pl.ANY)] * len(more),
        out_specs=pl.BlockSpec(memory_space=pl.ANY),
        out_shape=jax.ShapeDtypeStruct(base.shape, base.dtype),
        input_output_aliases={4: 0} if more else {},
        scratch_shapes=[
            pltpu.VMEM((len(blocks), HALF, WIDE), jnp.float32),
            pltpu.VMEM((len(blocks), HALF, WIDE), jnp.float32),
            pltpu.SemaphoreType.DMA((len(blocks),)),
            pltpu.SemaphoreType.DMA((len(blocks),)),
        ],
        name=f"apply_{half}",
    )(base, *updates, *more)


def turned(value, axis, dim):
    return jnp.where(lax.axis_index(axis) == 0, value, jnp.flip(value, dim))


def momentum_to_holders(momentum):
    rows = 2 * HALF
    m = momentum.astype(jnp.bfloat16).reshape(2, 2, rows, WIDE)
    m = turned(turned(m, "xh", 0), "c", 1)
    holder = {(column_plane(r, z, c), z, c): r for r in range(8) for z in range(8) for c in range(2)}
    moved = [send(m[dx], lambda r, z, xh, c: (holder[z, r, c], z, xh ^ dx, c)) for dx in range(2)]
    owner = {(r, column_plane(r, z, c), c): z for r in range(8) for z in range(8) for c in range(2)}
    m = send(jnp.stack(moved), lambda r, z, xh, c: (r, owner[r, z, c], xh, c))
    other = send(m[:, 1], lambda r, z, xh, c: (r, z, xh, 1 - c))
    return jnp.stack([m[:, 0], other]).reshape(8, HALF, WIDE)


def average_to_owners(average):
    average = average.reshape(2, 2, 2 * HALF, WIDE)
    other = send(average[1], lambda r, z, xh, c: (r, z, xh, 1 - c))
    moved = [
        send(
            jnp.stack([average[0, dx], other[dx]]),
            lambda r, z, xh, c: (z, column_plane(r, z, c), xh ^ dx, c),
        )
        for dx in range(2)
    ]
    return turned(turned(jnp.stack(moved), "c", 1), "xh", 0)


def per_device(local_weights, base_weights, momentum):
    count = lax.axis_size(R)
    local = local_weights[0]
    sums = list(deltas(local, base_weights, 1))
    held = momentum_to_holders(momentum)
    got = [exchange(sums[p], order[0]) for p, (order, _) in enumerate(PARTS)]
    kept = deltas(local, base_weights, 0)
    f32 = lambda v: v.astype(jnp.float32)
    total, averages, updates = [], [], []
    for p, (order, units) in enumerate(PARTS):
        total.append((f32(kept[p]) + f32(got[p])).reshape(2, 2, *kept[p].shape[1:]))
    for p, (order, units) in enumerate(PARTS):
        got[p] = exchange(total[p][1].astype(jnp.bfloat16), order[1])
    for p, (order, units) in enumerate(PARTS):
        total[p] = total[p][0] + f32(got[p])
        got[p] = exchange(total[p][1].astype(jnp.bfloat16), order[2])
    for p, (order, units) in enumerate(PARTS):
        average = (total[p][0] + f32(got[p])) * (1.0 / count)
        new = MOMENTUM_COEF * f32(held[units[0] : units[-1] + 1]) + average
        averages.append(average.astype(jnp.bfloat16))
        updates.append((LEARN_RATE * (average + MOMENTUM_COEF * new)).astype(jnp.bfloat16)[None])
    for p, (order, units) in enumerate(PARTS):
        updates[p] = jnp.concatenate([updates[p], exchange(updates[p], order[2])])
    returned = average_to_owners(jnp.concatenate(averages))
    for p, (order, units) in enumerate(PARTS):
        updates[p] = jnp.concatenate([updates[p], exchange(updates[p], order[1])])
    last = [exchange(updates[p], order[0]) for p, (order, _) in enumerate(PARTS)]
    new_momentum = MOMENTUM_COEF * momentum + f32(returned).reshape(momentum.shape)
    new_weights = apply_updates(base_weights, updates, 0, None)
    new_weights = apply_updates(base_weights, last, 1, new_weights)
    return new_weights, new_momentum


def solution(mesh):
    finer = Mesh(mesh.devices.reshape(4, 2, 8, 2, 2), EVERY)
    in_specs = (P(R, FSDP, None), P(FSDP, None), P(R, FSDP))
    out_specs = (P(FSDP, None), P(R, FSDP))
    return jax.shard_map(per_device, mesh=finer, in_specs=in_specs, out_specs=out_specs, check_vma=False)
```

time: 262 us -> 111 us (0.42)
  waiting for transfers between devices: 116 us -> 38.5 us
  local copies, waits for them, and re-layouts: 49.2 us -> 1.65 us
  blocking collectives: 25.6 us -> 0 us
  other arithmetic: 29.4 us -> 3.83 us
  Pallas kernels: 0 us -> 14.3 us
  starting transfers between devices: 40.8 us -> 49.4 us
    all_to_all x6 -> x0, waiting for transfers between devices: 116 us -> none  [the longest x4 52 us: turned_blocks(): filled = lax.all_to_all(filled, axes[k], k, k, tiled=True)]
    ppermute x0 -> x25, starting transfers between devices: none -> 49.4 us  [send(): return lax.ppermute(value, EVERY, pairs(there))]
    all_to_all x6 -> x0, starting transfers between devices: 40.8 us -> none  [the longest x4 23.1 us: turned_blocks(): filled = lax.all_to_all(filled, axes[k], k, k, tiled=True)]
    ppermute x0 -> x25, waiting for transfers between devices: none -> 38.5 us  [send(): return lax.ppermute(value, EVERY, pairs(there))]
    unnamed x22 -> x16, local copies, waits for them, and re-layouts: 27.9 us -> 1.5 us
    all_to_all x1 -> x0, blocking collectives: 25.6 us -> none  [copy_for_each(): return lax.all_to_all(copies, axis, split_axis=0, concat_axis=0, tiled=True)]
    unnamed x3 -> x0, other arithmetic: 18.6 us -> none
    pallas_call x0 -> x4, Pallas kernels: none -> 14.3 us  [the longest x2 7.66 us: apply_updates(): pl.pallas_call(body, in_specs=[pl.BlockSpec(memory_space=pl.ANY)] + [pl.B...]
  transfers between devices with their start and end apart: 6 -> 25, of which waited for: 5 -> 19; matrix products, arithmetic and copies ran while one was open for 8% -> 2% of each run, Pallas kernels for 0% -> 7%
where the time goes in v2:
time: 111 us; the launch traced here: 109 us
  starting transfers between devices  49.4 us (45%)
  waiting for transfers between devices  38.5 us (35%)
  Pallas kernels  14.3 us (13%)
  other arithmetic  3.83 us (3%)
  local copies, waits for them, and re-layouts  1.65 us (1%)
  between operations  1.14 us (1%)
    ppermute x25, starting transfers between devices, send(): return lax.ppermute(value, EVERY, pairs(there))  49.4 us
    ppermute x25, waiting for transfers between devices, send(): return lax.ppermute(value, EVERY, pairs(there))  38.5 us
    pallas_call x2, Pallas kernels, apply_updates(): pl.pallas_call(body, in_specs=[pl.BlockSpec(memory_space=pl.ANY)] + [pl.B...  7.66 us
    pallas_call x2, Pallas kernels, deltas(): pl.pallas_call(body, in_specs=[pl.BlockSpec(memory_space=pl.ANY)] * 2, ou...  6.62 us
  transfers between devices with their start and end apart: 25, of which 19 were waited for; matrix products, arithmetic and copies ran while one was open for 2% of the time, Pallas kernels for 7%

profile of v2, /device:TPU:1, one launch (start us, length us, event | category | flops | bytes accessed | tf_op | source)
XLA Modules:
  0.0 108.8 jit_solution(14815596369863462246)
XLA Ops:
  0.6 3.3 %delta_1.1 = (bf16[4,3,16,896]{3,2,1,0:T(8,128)(2,1)}, bf16[4,3,16,896]{3,2,1,0:T(8,128)(2,1)}, bf16[4,2,16,896]{3,2,1,0:T(8,128)(2,1)}) custom-call(bf16[32,28672]{1,0:T(8,128)(2,1)} %bitcast.75, f32[32,28672]{1,0:T(8,128)} %base_hbm.7), custom_call_target="tpu_custom_call" | custom-call | tf_op jit(solution)/shard_map/delta_1/pallas_call | solution.py:93
  4.0 3.6 %collective-permute-start.16 = (bf16[4,2,16,896]{3,2,1,0:T(8,128)(2,1)}, bf16[4,2,16,896]{3,2,1,0:T(8,128)(2,1)S(1)}, u32[]{:S(2)}, u32[]{:S(2)}) collective-permute-start(bf16[4,2,16,896]{3,2,1,0:T(8,128)(2,1)} %get-tuple-element.13), channel_id=1, source_target_pairs={{0,192},{1,193},{2,194},{3,195},{4,196},{5,197},{6,198},{7,199},{8... | collective-permute-start | bytes 688136 | tf_op jit(solution)/shard_map/ppermute | solution.py:41
  7.6 1.2 %collective-permute-start = (bf16[4,3,16,896]{3,2,1,0:T(8,128)(2,1)}, bf16[4,3,16,896]{3,2,1,0:T(8,128)(2,1)S(1)}, u32[]{:S(2)}, u32[]{:S(2)}) collective-permute-start(bf16[4,3,16,896]{3,2,1,0:T(8,128)(2,1)} %get-tuple-element.9), channel_id=1, source_target_pairs={{0,32},{1,33},{2,34},{3,35},{4,36},{5,37},{6,38},{7,39},{8,40},{9,... | collective-permute-start | bytes 1032200 | tf_op jit(solution)/shard_map/ppermute | solution.py:41
  8.8 3.3 %delta_0.1 = (bf16[4,3,16,896]{3,2,1,0:T(8,128)(2,1)}, bf16[4,3,16,896]{3,2,1,0:T(8,128)(2,1)}, bf16[4,2,16,896]{3,2,1,0:T(8,128)(2,1)}) custom-call(bf16[32,28672]{1,0:T(8,128)(2,1)} %bitcast.76, f32[32,28672]{1,0:T(8,128)} %base_hbm.7), custom_call_target="tpu_custom_call" | custom-call | tf_op jit(solution)/shard_map/delta_0/pallas_call | solution.py:93
  12.2 1.0 convert_add_fusion.3
  13.2 2.0 %collective-permute-start.17 = (bf16[2,2,16,896]{3,2,1,0:T(8,128)(2,1)S(1)}, bf16[2,2,16,896]{3,2,1,0:T(8,128)(2,1)S(1)}, u32[]{:S(2)}, u32[]{:S(2)}) collective-permute-start(bf16[2,2,16,896]{3,2,1,0:T(8,128)(2,1)S(1)} %slice.192), channel_id=1, source_target_pairs={{0,32},{1,33},{2,34},{3,35},{4,36},{5,37},{6,38},{7,39},{8,40},{9,... | collective-permute-start | bytes 344072 | tf_op jit(solution)/shard_map/ppermute | solution.py:41
  15.2 1.3 %collective-permute-done = bf16[4,3,16,896]{3,2,1,0:T(8,128)(2,1)S(1)} collective-permute-done((bf16[4,3,16,896]{3,2,1,0:T(8,128)(2,1)}, bf16[4,3,16,896]{3,2,1,0:T(8,128)(2,1)S(1)}, u32[]{:S(2)}, u32[]{:S(2)}) %collective-permute-start) | collective-permute-done | bytes 344096 | tf_op jit(solution)/shard_map/ppermute | solution.py:41
  16.5 1.0 convert_add_fusion.1
  17.7 1.3 %collective-permute-done.17 = bf16[2,2,16,896]{3,2,1,0:T(8,128)(2,1)S(1)} collective-permute-done((bf16[2,2,16,896]{3,2,1,0:T(8,128)(2,1)S(1)}, bf16[2,2,16,896]{3,2,1,0:T(8,128)(2,1)S(1)}, u32[]{:S(2)}, u32[]{:S(2)}) %collective-permute-start.17) | collective-permute-done | bytes 114720 | tf_op jit(solution)/shard_map/ppermute | solution.py:41
  19.0 0.3 collective-permute-start.18
  19.3 1.4 %collective-permute-start.11 = (bf16[2,3,16,896]{3,2,1,0:T(8,128)(2,1)S(1)}, bf16[2,3,16,896]{3,2,1,0:T(8,128)(2,1)S(1)}, u32[]{:S(2)}, u32[]{:S(2)}) collective-permute-start(bf16[2,3,16,896]{3,2,1,0:T(8,128)(2,1)S(1)} %slice.190), channel_id=1, source_target_pairs={{0,192},{1,193},{2,194},{3,195},{4,196},{5,197},{6,198},{7,199},{8... | collective-permute-start | bytes 516104 | tf_op jit(solution)/shard_map/ppermute | solution.py:41
  20.8 1.7 %collective-permute-done.18 = bf16[2,16,896]{2,1,0:T(8,128)(2,1)S(1)} collective-permute-done((bf16[2,16,896]{2,1,0:T(8,128)(2,1)S(1)}, bf16[2,16,896]{2,1,0:T(8,128)(2,1)S(1)}, u32[]{:S(2)}, u32[]{:S(2)}) %collective-permute-start.18) | collective-permute-done | bytes 57376 | tf_op jit(solution)/shard_map/ppermute | solution.py:41
  22.5 2.4 %collective-permute-done.11 = bf16[2,3,16,896]{3,2,1,0:T(8,128)(2,1)S(1)} collective-permute-done((bf16[2,3,16,896]{3,2,1,0:T(8,128)(2,1)S(1)}, bf16[2,3,16,896]{3,2,1,0:T(8,128)(2,1)S(1)}, u32[]{:S(2)}, u32[]{:S(2)}) %collective-permute-start.11) | collective-permute-done | bytes 172064 | tf_op jit(solution)/shard_map/ppermute | solution.py:41
  25.0 1.4 %collective-permute-start.12 = (bf16[3,16,896]{2,1,0:T(8,128)(2,1)S(1)}, bf16[3,16,896]{2,1,0:T(8,128)(2,1)S(1)}, u32[]{:S(2)}, u32[]{:S(2)}) collective-permute-start(bf16[3,16,896]{2,1,0:T(8,128)(2,1)S(1)} %fusion.11), channel_id=1, source_target_pairs={{0,32},{1,33},{2,34},{3,35},{4,36},{5,37},{6,38},{7,39},{8,40},{9,... | collective-permute-start | bytes 258056 | tf_op jit(solution)/shard_map/ppermute | solution.py:41
  26.4 1.2 %collective-permute-start.2 = (bf16[3,16,896]{2,1,0:T(8,128)(2,1)S(1)}, bf16[3,16,896]{2,1,0:T(8,128)(2,1)S(1)}, u32[]{:S(2)}, u32[]{:S(2)}) collective-permute-start(bf16[3,16,896]{2,1,0:T(8,128)(2,1)S(1)} %fusion.10), channel_id=1, source_target_pairs={{0,192},{1,193},{2,194},{3,195},{4,196},{5,197},{6,198},{7,199},{8... | collective-permute-start | bytes 258056 | tf_op jit(solution)/shard_map/ppermute | solution.py:41
  27.6 1.1 collective-permute-done.12
  28.7 2.3 %collective-permute-done.2 = bf16[3,16,896]{2,1,0:T(8,128)(2,1)S(1)} collective-permute-done((bf16[3,16,896]{2,1,0:T(8,128)(2,1)S(1)}, bf16[3,16,896]{2,1,0:T(8,128)(2,1)S(1)}, u32[]{:S(2)}, u32[]{:S(2)}) %collective-permute-start.2) | collective-permute-done | bytes 86048 | tf_op jit(solution)/shard_map/ppermute | solution.py:41
  31.1 6.1 %collective-permute-start.22 = (bf16[2,32,896]{2,1,0:T(8,128)(2,1)S(1)}, bf16[2,32,896]{2,1,0:T(8,128)(2,1)S(1)}, u32[]{:S(2)}, u32[]{:S(2)}) collective-permute-start(bf16[2,32,896]{2,1,0:T(8,128)(2,1)S(1)} %bitcast.86), channel_id=1, source_target_pairs={{0,1},{1,0},{2,3},{3,2},{4,5},{5,4},{6,7},{7,6},{8,9},{9,8},{10,11... | collective-permute-start | bytes 344072 | tf_op jit(solution)/shard_map/ppermute | solution.py:41
  37.3 1.0 collective-permute-done.22
  38.3 7.8 %collective-permute-start.24 = (bf16[2,32,896]{2,1,0:T(8,128)(2,1)S(1)}, bf16[2,32,896]{2,1,0:T(8,128)(2,1)S(1)}, u32[]{:S(2)}, u32[]{:S(2)}) collective-permute-start(bf16[2,32,896]{2,1,0:T(8,128)(2,1)S(1)} %pad_maximum_fusion.12), channel_id=1, source_target_pairs={{0,2},{1,31},{2,0},{3,29},{4,38},{5,59},{6,36},{7,57},{8,74},{9,87... | collective-permute-start | bytes 344072 | tf_op jit(solution)/shard_map/ppermute | solution.py:41
  46.1 1.9 %collective-permute-start.23 = (bf16[2,32,896]{2,1,0:T(8,128)(2,1)S(1)}, bf16[2,32,896]{2,1,0:T(8,128)(2,1)S(1)}, u32[]{:S(2)}, u32[]{:S(2)}) collective-permute-start(bf16[2,32,896]{2,1,0:T(8,128)(2,1)S(1)} %pad_maximum_fusion.11), channel_id=1, source_target_pairs={{0,0},{1,29},{2,2},{3,31},{4,36},{5,57},{6,38},{7,59},{8,72},{9,85... | collective-permute-start | bytes 344072 | tf_op jit(solution)/shard_map/ppermute | solution.py:41
  48.0 1.0 collective-permute-done.24
  49.0 4.7 %collective-permute-done.23 = bf16[2,32,896]{2,1,0:T(8,128)(2,1)S(1)} collective-permute-done((bf16[2,32,896]{2,1,0:T(8,128)(2,1)S(1)}, bf16[2,32,896]{2,1,0:T(8,128)(2,1)S(1)}, u32[]{:S(2)}, u32[]{:S(2)}) %collective-permute-start.23) | collective-permute-done | bytes 114720 | tf_op jit(solution)/shard_map/ppermute | solution.py:41
  53.9 0.8 convert_add_fusion.2
  54.9 1.9 %collective-permute-start.3 = (bf16[2,32,896]{2,1,0:T(8,128)(2,1)S(1)}, bf16[2,32,896]{2,1,0:T(8,128)(2,1)S(1)}, u32[]{:S(2)}, u32[]{:S(2)}) collective-permute-start(bf16[2,32,896]{2,1,0:T(8,128)(2,1)S(1)} %get-tuple-element.22), channel_id=1, source_target_pairs={{0,0},{1,225},{2,2},{3,227},{4,36},{5,197},{6,38},{7,199},{8,72},{... | collective-permute-start | bytes 344072 | tf_op jit(solution)/shard_map/ppermute | solution.py:41
  56.8 3.0 %collective-permute-start.4 = (bf16[2,32,896]{2,1,0:T(8,128)(2,1)S(1)}, bf16[2,32,896]{2,1,0:T(8,128)(2,1)S(1)}, u32[]{:S(2)}, u32[]{:S(2)}) collective-permute-start(bf16[2,32,896]{2,1,0:T(8,128)(2,1)S(1)} %get-tuple-element.23), channel_id=1, source_target_pairs={{0,2},{1,227},{2,0},{3,225},{4,38},{5,199},{6,36},{7,197},{8,74},{... | collective-permute-start | bytes 344072 | tf_op jit(solution)/shard_map/ppermute | solution.py:41
  59.8 4.1 %collective-permute-done.3 = bf16[2,32,896]{2,1,0:T(8,128)(2,1)S(1)} collective-permute-done((bf16[2,32,896]{2,1,0:T(8,128)(2,1)S(1)}, bf16[2,32,896]{2,1,0:T(8,128)(2,1)S(1)}, u32[]{:S(2)}, u32[]{:S(2)}) %collective-permute-start.3) | collective-permute-done | bytes 114720 | tf_op jit(solution)/shard_map/ppermute | solution.py:41
  63.9 0.5 collective-permute-done.4
  64.4 1.9 %collective-permute-start.5 = (bf16[2,2,32,896]{3,2,0,1:T(8,128)(2,1)S(1)}, bf16[2,2,32,896]{3,2,0,1:T(8,128)(2,1)S(1)}, u32[]{:S(2)}, u32[]{:S(2)}) collective-permute-start(bf16[2,2,32,896]{3,2,0,1:T(8,128)(2,1)S(1)} %pad_maximum_fusion.2), channel_id=1, source_target_pairs={{0,0},{1,29},{2,2},{3,31},{4,4},{5,25},{6,6},{7,27},{8,8},{9,21},{... | collective-permute-start | bytes 688136 | tf_op jit(solution)/shard_map/ppermute | solution.py:41
  66.4 8.5 %collective-permute-done.5 = bf16[2,2,32,896]{3,2,0,1:T(8,128)(2,1)S(1)} collective-permute-done((bf16[2,2,32,896]{3,2,0,1:T(8,128)(2,1)S(1)}, bf16[2,2,32,896]{3,2,0,1:T(8,128)(2,1)S(1)}, u32[]{:S(2)}, u32[]{:S(2)}) %collective-permute-start.5) | collective-permute-done | bytes 229408 | tf_op jit(solution)/shard_map/ppermute | solution.py:41
  74.9 0.1 collective-permute-start.6
  75.0 1.3 %collective-permute-done.6 = bf16[2,32,896]{2,1,0:T(8,128)(2,1)S(1)} collective-permute-done((bf16[2,32,896]{2,1,0:T(8,128)(2,1)S(1)}, bf16[2,32,896]{2,1,0:T(8,128)(2,1)S(1)}, u32[]{:S(2)}, u32[]{:S(2)}) %collective-permute-start.6) | collective-permute-done | bytes 114720 | tf_op jit(solution)/shard_map/ppermute | solution.py:41
  76.3 0.1 fusion.9
  76.4 7.2 %collective-permute-start.7 = (bf16[1,3,16,896]{3,2,1,0:T(8,128)(2,1)S(1)}, bf16[1,3,16,896]{3,2,1,0:T(8,128)(2,1)S(1)}, u32[]{:S(2)}, u32[]{:S(2)}) collective-permute-start(bf16[1,3,16,896]{3,2,1,0:T(8,128)(2,1)S(1)} %get-tuple-element.19), channel_id=1, source_target_pairs={{0,192},{1,193},{2,194},{3,195},{4,196},{5,197},{6,198},{7,199},{8... | collective-permute-start | bytes 258056 | tf_op jit(solution)/shard_map/ppermute | solution.py:41
  83.7 1.9 %collective-permute-start.19 = (bf16[1,2,16,896]{3,2,1,0:T(8,128)(2,1)S(1)}, bf16[1,2,16,896]{3,2,1,0:T(8,128)(2,1)S(1)}, u32[]{:S(2)}, u32[]{:S(2)}) collective-permute-start(bf16[1,2,16,896]{3,2,1,0:T(8,128)(2,1)S(1)} %fusion.13), channel_id=1, source_target_pairs={{0,64},{1,65},{2,66},{3,67},{4,68},{5,69},{6,70},{7,71},{8,72},{9,... | collective-permute-start | bytes 172040 | tf_op jit(solution)/shard_map/ppermute | solution.py:41
  85.5 0.6 collective-permute-done.7
  86.2 3.4 %collective-permute-start.8 = (bf16[2,3,16,896]{3,2,1,0:T(8,128)(2,1)S(1)}, bf16[2,3,16,896]{3,2,1,0:T(8,128)(2,1)S(1)}, u32[]{:S(2)}, u32[]{:S(2)}) collective-permute-start(bf16[2,3,16,896]{3,2,1,0:T(8,128)(2,1)S(1)} %pad_maximum_fusion.7), channel_id=1, source_target_pairs={{0,64},{1,65},{2,66},{3,67},{4,68},{5,69},{6,70},{7,71},{8,72},{9,... | collective-permute-start | bytes 516104 | tf_op jit(solution)/shard_map/ppermute | solution.py:41
  89.6 1.4 %collective-permute-start.14 = (bf16[2,3,16,896]{3,2,1,0:T(8,128)(2,1)S(1)}, bf16[2,3,16,896]{3,2,1,0:T(8,128)(2,1)S(1)}, u32[]{:S(2)}, u32[]{:S(2)}) collective-permute-start(bf16[2,3,16,896]{3,2,1,0:T(8,128)(2,1)S(1)} %pad_maximum_fusion.8), channel_id=1, source_target_pairs={{0,192},{1,193},{2,194},{3,195},{4,196},{5,197},{6,198},{7,199},{8... | collective-permute-start | bytes 516104 | tf_op jit(solution)/shard_map/ppermute | solution.py:41
  91.0 0.4 collective-permute-start.20
  91.5 1.9 %collective-permute-done.8 = bf16[2,3,16,896]{3,2,1,0:T(8,128)(2,1)S(1)} collective-permute-done((bf16[2,3,16,896]{3,2,1,0:T(8,128)(2,1)S(1)}, bf16[2,3,16,896]{3,2,1,0:T(8,128)(2,1)S(1)}, u32[]{:S(2)}, u32[]{:S(2)}) %collective-permute-start.8) | collective-permute-done | bytes 172064 | tf_op jit(solution)/shard_map/ppermute | solution.py:41
  93.5 2.1 %collective-permute-done.14 = bf16[2,3,16,896]{3,2,1,0:T(8,128)(2,1)S(1)} collective-permute-done((bf16[2,3,16,896]{3,2,1,0:T(8,128)(2,1)S(1)}, bf16[2,3,16,896]{3,2,1,0:T(8,128)(2,1)S(1)}, u32[]{:S(2)}, u32[]{:S(2)}) %collective-permute-start.14) | collective-permute-done | bytes 172064 | tf_op jit(solution)/shard_map/ppermute | solution.py:41
  95.8 1.0 collective-permute-start.21
  96.8 3.8 %apply_0.1.refs_3_ = f32[32,28672]{1,0:T(8,128)} custom-call(f32[32,28672]{1,0:T(8,128)} %base_hbm.7, bf16[4,3,16,896]{3,2,1,0:T(8,128)(2,1)} %copy-done, bf16[4,3,16,896]{3,2,1,0:T(8,128)(2,1)} %copy-done.1, bf16[4,2,16,896]{3,2,1,0:T(8,128)(2,1)} %copy-done.2), custom_call_target="tpu_custom_call" | custom-call | tf_op jit(solution)/shard_map/apply_0/pallas_call | solution.py:130
  100.6 1.3 %collective-permute-done.21.refs_2_ = bf16[4,2,16,896]{3,2,1,0:T(8,128)(2,1)S(1)} collective-permute-done((bf16[4,2,16,896]{3,2,1,0:T(8,128)(2,1)S(1)}, bf16[4,2,16,896]{3,2,1,0:T(8,128)(2,1)S(1)}, u32[]{:S(2)}, u32[]{:S(2)}) %collective-permute-start.21) | collective-permute-done | bytes 229408 | tf_op jit(solution)/shard_map/ppermute | solution.py:41
  102.0 1.4 %collective-permute-done.9.refs_0_ = bf16[4,3,16,896]{3,2,1,0:T(8,128)(2,1)S(1)} collective-permute-done((bf16[4,3,16,896]{3,2,1,0:T(8,128)(2,1)S(1)}, bf16[4,3,16,896]{3,2,1,0:T(8,128)(2,1)S(1)}, u32[]{:S(2)}, u32[]{:S(2)}) %collective-permute-start.9) | collective-permute-done | bytes 344096 | tf_op jit(solution)/shard_map/ppermute | solution.py:41
  103.3 0.7 copy-done.4
  104.1 0.7 copy-done.5
  104.8 3.8 %apply_1.1 = f32[32,28672]{1,0:T(8,128)} custom-call(f32[32,28672]{1,0:T(8,128)} %base_hbm.7, bf16[4,3,16,896]{3,2,1,0:T(8,128)(2,1)} %copy-done.4, bf16[4,3,16,896]{3,2,1,0:T(8,128)(2,1)} %copy-done.5, bf16[4,2,16,896]{3,2,1,0:T(8,128)(2,1)} %copy-done.7, f32[32,28672]{1,0:T(8,128)} %apply_0.1.refs_3_), custom_call_target="tpu_custom_call", output_to_operand_aliasing={{}: (4, {})} | custom-call | tf_op jit(solution)/shard_map/apply_1/pallas_call | solution.py:130
  (61 shorter events, 1.4 us)
Async XLA Ops:
  4.0 8.2 %collective-permute-start.16 = (bf16[4,2,16,896]{3,2,1,0:T(8,128)(2,1)}, bf16[4,2,16,896]{3,2,1,0:T(8,128)(2,1)S(1)}, u32[]{:S(2)}, u32[]{:S(2)}) collective-permute-start(bf16[4,2,16,896]{3,2,1,0:T(8,128)(2,1)} %get-tuple-element.13), channel_id=1, source_target_pairs={{0,192},{1,193},{2,194},{3,195},{4,196},{5,197},{6,198},{7,199},{8... | collective-permute-start | bytes 688136 | tf_op jit(solution)/shard_map/ppermute | solution.py:41
  7.6 8.9 %collective-permute-start = (bf16[4,3,16,896]{3,2,1,0:T(8,128)(2,1)}, bf16[4,3,16,896]{3,2,1,0:T(8,128)(2,1)S(1)}, u32[]{:S(2)}, u32[]{:S(2)}) collective-permute-start(bf16[4,3,16,896]{3,2,1,0:T(8,128)(2,1)} %get-tuple-element.9), channel_id=1, source_target_pairs={{0,32},{1,33},{2,34},{3,35},{4,36},{5,37},{6,38},{7,39},{8,40},{9,... | collective-permute-start | bytes 1032200 | tf_op jit(solution)/shard_map/ppermute | solution.py:41
  8.8 10.4 %collective-permute-start.10 = (bf16[4,3,16,896]{3,2,1,0:T(8,128)(2,1)}, bf16[4,3,16,896]{3,2,1,0:T(8,128)(2,1)S(1)}, u32[]{:S(2)}, u32[]{:S(2)}) collective-permute-start(bf16[4,3,16,896]{3,2,1,0:T(8,128)(2,1)} %get-tuple-element.11), channel_id=1, source_target_pairs={{0,64},{1,65},{2,66},{3,67},{4,68},{5,69},{6,70},{7,71},{8,72},{9,... | collective-permute-start | bytes 1032200 | tf_op jit(solution)/shard_map/ppermute | solution.py:41
  12.1 7.1 %copy-start.6 = (bf16[4,3,16,896]{3,2,1,0:T(8,128)(2,1)S(1)}, bf16[4,3,16,896]{3,2,1,0:T(8,128)(2,1)}, u32[]{:S(2)}) copy-start(bf16[4,3,16,896]{3,2,1,0:T(8,128)(2,1)} %get-tuple-element.10) | copy-start | bytes 1032196
  13.2 5.7 %collective-permute-start.17 = (bf16[2,2,16,896]{3,2,1,0:T(8,128)(2,1)S(1)}, bf16[2,2,16,896]{3,2,1,0:T(8,128)(2,1)S(1)}, u32[]{:S(2)}, u32[]{:S(2)}) collective-permute-start(bf16[2,2,16,896]{3,2,1,0:T(8,128)(2,1)S(1)} %slice.192), channel_id=1, source_target_pairs={{0,32},{1,33},{2,34},{3,35},{4,36},{5,37},{6,38},{7,39},{8,40},{9,... | collective-permute-start | bytes 344072 | tf_op jit(solution)/shard_map/ppermute | solution.py:41
  17.6 8.8 %collective-permute-start.1 = (bf16[2,3,16,896]{3,2,1,0:T(8,128)(2,1)S(1)}, bf16[2,3,16,896]{3,2,1,0:T(8,128)(2,1)S(1)}, u32[]{:S(2)}, u32[]{:S(2)}) collective-permute-start(bf16[2,3,16,896]{3,2,1,0:T(8,128)(2,1)S(1)} %slice.191), channel_id=1, source_target_pairs={{0,64},{1,65},{2,66},{3,67},{4,68},{5,69},{6,70},{7,71},{8,72},{9,... | collective-permute-start | bytes 516104 | tf_op jit(solution)/shard_map/ppermute | solution.py:41
  19.0 3.5 %collective-permute-start.18 = (bf16[2,16,896]{2,1,0:T(8,128)(2,1)S(1)}, bf16[2,16,896]{2,1,0:T(8,128)(2,1)S(1)}, u32[]{:S(2)}, u32[]{:S(2)}) collective-permute-start(bf16[2,16,896]{2,1,0:T(8,128)(2,1)S(1)} %fusion.14), channel_id=1, source_target_pairs={{0,64},{1,65},{2,66},{3,67},{4,68},{5,69},{6,70},{7,71},{8,72},{9,... | collective-permute-start | bytes 172040 | tf_op jit(solution)/shard_map/ppermute | solution.py:41
  19.2 34.6 %copy-start.3 = (f32[128,896]{1,0:T(8,128)S(1)}, f32[128,896]{1,0:T(8,128)}, u32[]{:S(2)}) copy-start(f32[128,896]{1,0:T(8,128)} %param.5) | copy-start | bytes 1376260
  19.3 5.6 %collective-permute-start.11 = (bf16[2,3,16,896]{3,2,1,0:T(8,128)(2,1)S(1)}, bf16[2,3,16,896]{3,2,1,0:T(8,128)(2,1)S(1)}, u32[]{:S(2)}, u32[]{:S(2)}) collective-permute-start(bf16[2,3,16,896]{3,2,1,0:T(8,128)(2,1)S(1)} %slice.190), channel_id=1, source_target_pairs={{0,192},{1,193},{2,194},{3,195},{4,196},{5,197},{6,198},{7,199},{8... | collective-permute-start | bytes 516104 | tf_op jit(solution)/shard_map/ppermute | solution.py:41
  25.0 3.7 %collective-permute-start.12 = (bf16[3,16,896]{2,1,0:T(8,128)(2,1)S(1)}, bf16[3,16,896]{2,1,0:T(8,128)(2,1)S(1)}, u32[]{:S(2)}, u32[]{:S(2)}) collective-permute-start(bf16[3,16,896]{2,1,0:T(8,128)(2,1)S(1)} %fusion.11), channel_id=1, source_target_pairs={{0,32},{1,33},{2,34},{3,35},{4,36},{5,37},{6,38},{7,39},{8,40},{9,... | collective-permute-start | bytes 258056 | tf_op jit(solution)/shard_map/ppermute | solution.py:41
  26.4 4.6 %collective-permute-start.2 = (bf16[3,16,896]{2,1,0:T(8,128)(2,1)S(1)}, bf16[3,16,896]{2,1,0:T(8,128)(2,1)S(1)}, u32[]{:S(2)}, u32[]{:S(2)}) collective-permute-start(bf16[3,16,896]{2,1,0:T(8,128)(2,1)S(1)} %fusion.10), channel_id=1, source_target_pairs={{0,192},{1,193},{2,194},{3,195},{4,196},{5,197},{6,198},{7,199},{8... | collective-permute-start | bytes 258056 | tf_op jit(solution)/shard_map/ppermute | solution.py:41
  31.1 7.1 %collective-permute-start.22 = (bf16[2,32,896]{2,1,0:T(8,128)(2,1)S(1)}, bf16[2,32,896]{2,1,0:T(8,128)(2,1)S(1)}, u32[]{:S(2)}, u32[]{:S(2)}) collective-permute-start(bf16[2,32,896]{2,1,0:T(8,128)(2,1)S(1)} %bitcast.86), channel_id=1, source_target_pairs={{0,1},{1,0},{2,3},{3,2},{4,5},{5,4},{6,7},{7,6},{8,9},{9,8},{10,11... | collective-permute-start | bytes 344072 | tf_op jit(solution)/shard_map/ppermute | solution.py:41
  38.3 10.8 %collective-permute-start.24 = (bf16[2,32,896]{2,1,0:T(8,128)(2,1)S(1)}, bf16[2,32,896]{2,1,0:T(8,128)(2,1)S(1)}, u32[]{:S(2)}, u32[]{:S(2)}) collective-permute-start(bf16[2,32,896]{2,1,0:T(8,128)(2,1)S(1)} %pad_maximum_fusion.12), channel_id=1, source_target_pairs={{0,2},{1,31},{2,0},{3,29},{4,38},{5,59},{6,36},{7,57},{8,74},{9,87... | collective-permute-start | bytes 344072 | tf_op jit(solution)/shard_map/ppermute | solution.py:41
  46.1 7.6 %collective-permute-start.23 = (bf16[2,32,896]{2,1,0:T(8,128)(2,1)S(1)}, bf16[2,32,896]{2,1,0:T(8,128)(2,1)S(1)}, u32[]{:S(2)}, u32[]{:S(2)}) collective-permute-start(bf16[2,32,896]{2,1,0:T(8,128)(2,1)S(1)} %pad_maximum_fusion.11), channel_id=1, source_target_pairs={{0,0},{1,29},{2,2},{3,31},{4,36},{5,57},{6,38},{7,59},{8,72},{9,85... | collective-permute-start | bytes 344072 | tf_op jit(solution)/shard_map/ppermute | solution.py:41
  54.9 9.0 %collective-permute-start.3 = (bf16[2,32,896]{2,1,0:T(8,128)(2,1)S(1)}, bf16[2,32,896]{2,1,0:T(8,128)(2,1)S(1)}, u32[]{:S(2)}, u32[]{:S(2)}) collective-permute-start(bf16[2,32,896]{2,1,0:T(8,128)(2,1)S(1)} %get-tuple-element.22), channel_id=1, source_target_pairs={{0,0},{1,225},{2,2},{3,227},{4,36},{5,197},{6,38},{7,199},{8,72},{... | collective-permute-start | bytes 344072 | tf_op jit(solution)/shard_map/ppermute | solution.py:41
  56.8 7.6 %collective-permute-start.4 = (bf16[2,32,896]{2,1,0:T(8,128)(2,1)S(1)}, bf16[2,32,896]{2,1,0:T(8,128)(2,1)S(1)}, u32[]{:S(2)}, u32[]{:S(2)}) collective-permute-start(bf16[2,32,896]{2,1,0:T(8,128)(2,1)S(1)} %get-tuple-element.23), channel_id=1, source_target_pairs={{0,2},{1,227},{2,0},{3,225},{4,38},{5,199},{6,36},{7,197},{8,74},{... | collective-permute-start | bytes 344072 | tf_op jit(solution)/shard_map/ppermute | solution.py:41
  64.4 10.4 %collective-permute-start.5 = (bf16[2,2,32,896]{3,2,0,1:T(8,128)(2,1)S(1)}, bf16[2,2,32,896]{3,2,0,1:T(8,128)(2,1)S(1)}, u32[]{:S(2)}, u32[]{:S(2)}) collective-permute-start(bf16[2,2,32,896]{3,2,0,1:T(8,128)(2,1)S(1)} %pad_maximum_fusion.2), channel_id=1, source_target_pairs={{0,0},{1,29},{2,2},{3,31},{4,4},{5,25},{6,6},{7,27},{8,8},{9,21},{... | collective-permute-start | bytes 688136 | tf_op jit(solution)/shard_map/ppermute | solution.py:41
  74.9 1.4 %collective-permute-start.6 = (bf16[2,32,896]{2,1,0:T(8,128)(2,1)S(1)}, bf16[2,32,896]{2,1,0:T(8,128)(2,1)S(1)}, u32[]{:S(2)}, u32[]{:S(2)}) collective-permute-start(bf16[2,32,896]{2,1,0:T(8,128)(2,1)S(1)} %get-tuple-element.21), channel_id=1, source_target_pairs={{0,1},{1,0},{2,3},{3,2},{4,5},{5,4},{6,7},{7,6},{8,9},{9,8},{10,11... | collective-permute-start | bytes 344072 | tf_op jit(solution)/shard_map/ppermute | solution.py:41
  76.4 9.7 %collective-permute-start.7 = (bf16[1,3,16,896]{3,2,1,0:T(8,128)(2,1)S(1)}, bf16[1,3,16,896]{3,2,1,0:T(8,128)(2,1)S(1)}, u32[]{:S(2)}, u32[]{:S(2)}) collective-permute-start(bf16[1,3,16,896]{3,2,1,0:T(8,128)(2,1)S(1)} %get-tuple-element.19), channel_id=1, source_target_pairs={{0,192},{1,193},{2,194},{3,195},{4,196},{5,197},{6,198},{7,199},{8... | collective-permute-start | bytes 258056 | tf_op jit(solution)/shard_map/ppermute | solution.py:41
  83.7 7.4 %collective-permute-start.19 = (bf16[1,2,16,896]{3,2,1,0:T(8,128)(2,1)S(1)}, bf16[1,2,16,896]{3,2,1,0:T(8,128)(2,1)S(1)}, u32[]{:S(2)}, u32[]{:S(2)}) collective-permute-start(bf16[1,2,16,896]{3,2,1,0:T(8,128)(2,1)S(1)} %fusion.13), channel_id=1, source_target_pairs={{0,64},{1,65},{2,66},{3,67},{4,68},{5,69},{6,70},{7,71},{8,72},{9,... | collective-permute-start | bytes 172040 | tf_op jit(solution)/shard_map/ppermute | solution.py:41
  85.5 4.1 %collective-permute-start.13 = (bf16[1,3,16,896]{3,2,1,0:T(8,128)(2,1)S(1)}, bf16[1,3,16,896]{3,2,1,0:T(8,128)(2,1)S(1)}, u32[]{:S(2)}, u32[]{:S(2)}) collective-permute-start(bf16[1,3,16,896]{3,2,1,0:T(8,128)(2,1)S(1)} %get-tuple-element.18), channel_id=1, source_target_pairs={{0,32},{1,33},{2,34},{3,35},{4,36},{5,37},{6,38},{7,39},{8,40},{9,... | collective-permute-start | bytes 258056 | tf_op jit(solution)/shard_map/ppermute | solution.py:41
  86.2 7.1 %collective-permute-start.8 = (bf16[2,3,16,896]{3,2,1,0:T(8,128)(2,1)S(1)}, bf16[2,3,16,896]{3,2,1,0:T(8,128)(2,1)S(1)}, u32[]{:S(2)}, u32[]{:S(2)}) collective-permute-start(bf16[2,3,16,896]{3,2,1,0:T(8,128)(2,1)S(1)} %pad_maximum_fusion.7), channel_id=1, source_target_pairs={{0,64},{1,65},{2,66},{3,67},{4,68},{5,69},{6,70},{7,71},{8,72},{9,... | collective-permute-start | bytes 516104 | tf_op jit(solution)/shard_map/ppermute | solution.py:41
  89.6 5.9 %collective-permute-start.14 = (bf16[2,3,16,896]{3,2,1,0:T(8,128)(2,1)S(1)}, bf16[2,3,16,896]{3,2,1,0:T(8,128)(2,1)S(1)}, u32[]{:S(2)}, u32[]{:S(2)}) collective-permute-start(bf16[2,3,16,896]{3,2,1,0:T(8,128)(2,1)S(1)} %pad_maximum_fusion.8), channel_id=1, source_target_pairs={{0,192},{1,193},{2,194},{3,195},{4,196},{5,197},{6,198},{7,199},{8... | collective-permute-start | bytes 516104 | tf_op jit(solution)/shard_map/ppermute | solution.py:41
  91.0 4.7 %collective-permute-start.20 = (bf16[2,2,16,896]{3,2,1,0:T(8,128)(2,1)S(1)}, bf16[2,2,16,896]{3,2,1,0:T(8,128)(2,1)S(1)}, u32[]{:S(2)}, u32[]{:S(2)}) collective-permute-start(bf16[2,2,16,896]{3,2,1,0:T(8,128)(2,1)S(1)} %pad_maximum_fusion.10), channel_id=1, source_target_pairs={{0,32},{1,33},{2,34},{3,35},{4,36},{5,37},{6,38},{7,39},{8,40},{9,... | collective-permute-start | bytes 344072 | tf_op jit(solution)/shard_map/ppermute | solution.py:41
  93.4 3.4 %copy-start = (bf16[4,3,16,896]{3,2,1,0:T(8,128)(2,1)}, bf16[4,3,16,896]{3,2,1,0:T(8,128)(2,1)S(1)}, u32[]{:S(2)}) copy-start(bf16[4,3,16,896]{3,2,1,0:T(8,128)(2,1)S(1)} %pad_maximum_fusion.refs_0_) | copy-start | bytes 1032196
  93.4 9.9 %collective-permute-start.9 = (bf16[4,3,16,896]{3,2,1,0:T(8,128)(2,1)S(1)}, bf16[4,3,16,896]{3,2,1,0:T(8,128)(2,1)S(1)}, u32[]{:S(2)}, u32[]{:S(2)}) collective-permute-start(bf16[4,3,16,896]{3,2,1,0:T(8,128)(2,1)S(1)} %pad_maximum_fusion.refs_0_), channel_id=1, source_target_pairs={{0,32},{1,33},{2,34},{3,35},{4,36},{5,37},{6,38},{7,39},{8,40},{9,... | collective-permute-start | bytes 1032200 | tf_op jit(solution)/shard_map/ppermute | solution.py:41
  95.6 1.2 %copy-start.1 = (bf16[4,3,16,896]{3,2,1,0:T(8,128)(2,1)}, bf16[4,3,16,896]{3,2,1,0:T(8,128)(2,1)S(1)}, u32[]{:S(2)}) copy-start(bf16[4,3,16,896]{3,2,1,0:T(8,128)(2,1)S(1)} %pad_maximum_fusion.1.refs_1_) | copy-start | bytes 1032196
  95.6 7.7 %collective-permute-start.15 = (bf16[4,3,16,896]{3,2,1,0:T(8,128)(2,1)S(1)}, bf16[4,3,16,896]{3,2,1,0:T(8,128)(2,1)S(1)}, u32[]{:S(2)}, u32[]{:S(2)}) collective-permute-start(bf16[4,3,16,896]{3,2,1,0:T(8,128)(2,1)S(1)} %pad_maximum_fusion.1.refs_1_), channel_id=1, source_target_pairs={{0,64},{1,65},{2,66},{3,67},{4,68},{5,69},{6,70},{7,71},{8,72},{9,... | collective-permute-start | bytes 1032200 | tf_op jit(solution)/shard_map/ppermute | solution.py:41
  95.8 1.0 copy-start.2
  95.8 6.2 %collective-permute-start.21 = (bf16[4,2,16,896]{3,2,1,0:T(8,128)(2,1)S(1)}, bf16[4,2,16,896]{3,2,1,0:T(8,128)(2,1)S(1)}, u32[]{:S(2)}, u32[]{:S(2)}) collective-permute-start(bf16[4,2,16,896]{3,2,1,0:T(8,128)(2,1)S(1)} %pad_maximum_fusion.4.refs_2_), channel_id=1, source_target_pairs={{0,192},{1,193},{2,194},{3,195},{4,196},{5,197},{6,198},{7,199},{8... | collective-permute-start | bytes 688136 | tf_op jit(solution)/shard_map/ppermute | solution.py:41
  102.0 1.4 %copy-start.7 = (bf16[4,2,16,896]{3,2,1,0:T(8,128)(2,1)}, bf16[4,2,16,896]{3,2,1,0:T(8,128)(2,1)S(1)}, u32[]{:S(2)}) copy-start(bf16[4,2,16,896]{3,2,1,0:T(8,128)(2,1)S(1)} %collective-permute-done.21.refs_2_) | copy-start | bytes 688132
  103.3 0.7 copy-start.4
  104.1 0.7 copy-start.5

commit v3 on v2

v3 whole, which is shorter than its diff:
```python
import jax
import jax.numpy as jnp
from jax import lax
from jax.experimental import pallas as pl
from jax.experimental.pallas import tpu as pltpu
from jax.sharding import Mesh
from jax.sharding import PartitionSpec as P


R = ("y", "xl")
FSDP = ("z", "xh", "c")
EVERY = R + FSDP
LEARN_RATE = 0.7
MOMENTUM_COEF = 0.9
HALF = 16
WIDE = 896
VMEM_LIMIT = 12 << 20

MASKS = {"x": 1, "a": 2, "b": 6}
PARTS = (("xab", (0, 1, 2)), ("abx", (3, 4, 5)), ("bxa", (6, 7)))


def column_plane(r, z, c):
    return r ^ z ^ (7 * c)


def device(r, z, xh, c):
    return ((r * 8 + z) * 2 + xh) * 2 + c


def pairs(there):
    found = []
    for r in range(8):
        for z in range(8):
            for xh in range(2):
                for c in range(2):
                    found.append((device(r, z, xh, c), device(*there(r, z, xh, c))))
    return found


def send(value, there):
    return lax.ppermute(value, EVERY, pairs(there))


def exchange(value, dim):
    return send(value, lambda r, z, xh, c: (r ^ MASKS[dim], z, xh, c))


def in_vmem(value):
    return pltpu.with_memory_space_constraint(value, pltpu.VMEM)


def peer(order, first, second, third):
    return (first * MASKS[order[0]]) ^ (second * MASKS[order[1]]) ^ (third * MASKS[order[2]])


def blocks_of(half):
    listed = []
    for p, (order, units) in enumerate(PARTS):
        for second in range(2):
            for third in range(2):
                for n, unit in enumerate(units):
                    listed.append((p, (second * 2 + third, n), peer(order, half, second, third), unit))
    return listed


def place_of(peer_index, unit):
    r = lax.axis_index(R) ^ peer_index
    z, xh, c = lax.axis_index("z"), lax.axis_index("xh"), lax.axis_index("c")
    core = c ^ (unit // 4)
    column = 4 * column_plane(r, z, core) + 2 * (xh ^ (unit // 2 % 2)) + core
    return HALF * (unit % 2), pl.multiple_of(column * WIDE, 128)


def shapes_of():
    return [(4, len(units), HALF, WIDE) for _, units in PARTS]


def deltas(local, base, momentum, half):
    blocks = blocks_of(half)
    count = len(blocks)
    lead = 2 if momentum is not None else 0
    rows = 2 * HALF

    def body(*refs):
        local_hbm, base_hbm, *refs = refs
        if lead:
            old_hbm, *refs = refs
        outs, base_buf, refs = refs[:3], refs[3], refs[4:]
        if lead:
            moved, old_buf, refs = refs[:2], refs[2], refs[3:]
        local_buf, local_sem, base_sem = refs[:3]
        copies = []
        for n, (_, _, k, unit) in enumerate(blocks):
            row, col = place_of(k, unit)
            here = (pl.ds(row, HALF), pl.ds(col, WIDE))
            one = pltpu.make_async_copy(base_hbm.at[here], base_buf.at[n], base_sem.at[n])
            two = pltpu.make_async_copy(local_hbm.at[here], local_buf.at[n], local_sem.at[n])
            one.start()
            two.start()
            copies.append((one, two))
        if lead:
            old_sem = refs[3]
            xh, c = lax.axis_index("xh"), lax.axis_index("c")
            old_copies = []
            for dx in range(2):
                for dc in range(2):
                    row = pl.multiple_of(rows * (2 * (xh ^ dx) + (c ^ dc)), rows)
                    copy = pltpu.make_async_copy(
                        old_hbm.at[pl.ds(row, rows)], old_buf.at[dx, dc], old_sem.at[dx, dc]
                    )
                    copy.start()
                    old_copies.append((dx, dc, copy))
        for n, (p, at, _, _) in enumerate(blocks):
            for copy in copies[n]:
                copy.wait()
            outs[p][at] = (base_buf[n] - local_buf[n].astype(jnp.float32)).astype(jnp.bfloat16)
        if lead:
            for dx, dc, copy in old_copies:
                copy.wait()
                moved[dx][dc] = old_buf[dx, dc].astype(jnp.bfloat16)

    more = [momentum] if lead else []
    out_shape = [pltpu.VMEM(shape, jnp.bfloat16) for shape in shapes_of()]
    out_shape.append(pltpu.VMEM((count, HALF, WIDE), jnp.float32))
    scratch = [
        pltpu.VMEM((count, HALF, WIDE), jnp.bfloat16),
        pltpu.SemaphoreType.DMA((count,)),
        pltpu.SemaphoreType.DMA((count,)),
    ]
    if lead:
        out_shape += [pltpu.VMEM((2, rows, WIDE), jnp.bfloat16)] * 2
        out_shape.append(pltpu.VMEM((2, 2, rows, WIDE), jnp.float32))
        scratch.append(pltpu.SemaphoreType.DMA((2, 2)))
    return pl.pallas_call(
        body,
        in_specs=[pl.BlockSpec(memory_space=pltpu.HBM)] * (2 + len(more)),
        out_specs=[pl.BlockSpec(memory_space=pltpu.VMEM)] * len(out_shape),
        out_shape=out_shape,
        scratch_shapes=scratch,
        compiler_params=pltpu.CompilerParams(vmem_limit_bytes=VMEM_LIMIT),
    )(*[pltpu.with_memory_space_constraint(v, pltpu.HBM) for v in (local, base, *more)])


def apply_updates(base_blocks, updates, half, shape, earlier):
    blocks = blocks_of(half)

    def body(base_buf, *refs):
        parts, out_hbm, out_buf, out_sem = refs[:3], refs[-3], refs[-2], refs[-1]
        copies = []
        for n, (p, at, k, unit) in enumerate(blocks):
            row, col = place_of(k, unit)
            out_buf[n] = base_buf[n] - parts[p][at].astype(jnp.float32)
            there = out_hbm.at[pl.ds(row, HALF), pl.ds(col, WIDE)]
            copy = pltpu.make_async_copy(out_buf.at[n], there, out_sem.at[n])
            copy.start()
            copies.append(copy)
        for copy in copies:
            copy.wait()

    more = [] if earlier is None else [earlier]
    return pl.pallas_call(
        body,
        in_specs=[pl.BlockSpec(memory_space=pltpu.VMEM)] * 4
        + [pl.BlockSpec(memory_space=pltpu.HBM)] * len(more),
        out_specs=pl.BlockSpec(memory_space=pltpu.HBM),
        out_shape=jax.ShapeDtypeStruct(shape, jnp.float32),
        input_output_aliases={4: 0} if more else {},
        scratch_shapes=[
            pltpu.VMEM((len(blocks), HALF, WIDE), jnp.float32),
            pltpu.SemaphoreType.DMA((len(blocks),)),
        ],
        compiler_params=pltpu.CompilerParams(vmem_limit_bytes=VMEM_LIMIT),
    )(in_vmem(base_blocks), *[in_vmem(u) for u in updates], *more)


def next_momentum(old, returned, shape):
    rows = 2 * HALF

    def body(old_buf, *refs):
        pieces, out_hbm, out_buf, out_sem = refs[:2], refs[2], refs[3], refs[4]
        xh, c = lax.axis_index("xh"), lax.axis_index("c")
        copies = []
        for dx in range(2):
            for dc in range(2):
                row = pl.multiple_of(rows * (2 * (xh ^ dx) + (c ^ dc)), rows)
                out_buf[dx, dc] = MOMENTUM_COEF * old_buf[dx, dc] + pieces[dx][dc].astype(jnp.float32)
                copy = pltpu.make_async_copy(
                    out_buf.at[dx, dc], out_hbm.at[pl.ds(row, rows)], out_sem.at[dx, dc]
                )
                copy.start()
                copies.append(copy)
        for copy in copies:
            copy.wait()

    return pl.pallas_call(
        body,
        in_specs=[pl.BlockSpec(memory_space=pltpu.VMEM)] * 3,
        out_specs=pl.BlockSpec(memory_space=pltpu.HBM),
        out_shape=jax.ShapeDtypeStruct(shape, jnp.float32),
        scratch_shapes=[pltpu.VMEM(old.shape, jnp.float32), pltpu.SemaphoreType.DMA((2, 2))],
        compiler_params=pltpu.CompilerParams(vmem_limit_bytes=VMEM_LIMIT),
        name="momentum",
    )(in_vmem(old), *[in_vmem(v) for v in returned])


def momentum_to_holders(m):
    holder = {(column_plane(r, z, c), z, c): r for r in range(8) for z in range(8) for c in range(2)}
    moved = [send(m[dx], lambda r, z, xh, c: (holder[z, r, c], z, xh ^ dx, c)) for dx in range(2)]
    owner = {(r, column_plane(r, z, c), c): z for r in range(8) for z in range(8) for c in range(2)}
    m = send(jnp.stack(moved), lambda r, z, xh, c: (r, owner[r, z, c], xh, c))
    other = send(m[:, 1], lambda r, z, xh, c: (r, z, xh, 1 - c))
    return jnp.stack([m[:, 0], other]).reshape(8, HALF, WIDE)


def average_to_owners(average):
    average = average.reshape(2, 2, 2 * HALF, WIDE)
    other = send(average[1], lambda r, z, xh, c: (r, z, xh, 1 - c))
    return [
        send(
            jnp.stack([average[0, dx], other[dx]]),
            lambda r, z, xh, c: (z, column_plane(r, z, c), xh ^ dx, c),
        )
        for dx in range(2)
    ]


def f32(value):
    return value.astype(jnp.float32)


def b16(value):
    return value.astype(jnp.bfloat16)


def per_device(local_weights, base_weights, momentum):
    return outer_step(local_weights[0], base_weights, momentum)


def outer_step(local, base, momentum):
    count = lax.axis_size(R)
    *sends, base_1, m_0, m_1, old = deltas(local, base, momentum, 1)
    held = momentum_to_holders([m_0, m_1])
    first = [exchange(sends[p], order[0]) for p, (order, _) in enumerate(PARTS)]
    *kept, base_0 = deltas(local, base, None, 0)
    second, third, averages, updates = [], [], [], []
    for p, (order, units) in enumerate(PARTS):
        out = b16(f32(kept[p][2:]) + f32(first[p][2:]))
        second.append(exchange(out, order[1]))
    for p, (order, units) in enumerate(PARTS):
        out = b16(f32(kept[p][1]) + f32(first[p][1]) + f32(second[p][1]))
        third.append(exchange(out, order[2]))
    for p, (order, units) in enumerate(PARTS):
        total = f32(kept[p][0]) + f32(first[p][0]) + f32(second[p][0]) + f32(third[p])
        average = total * (1.0 / count)
        new = MOMENTUM_COEF * f32(held[units[0] : units[-1] + 1]) + average
        averages.append(b16(average))
        updates.append(b16(LEARN_RATE * (average + MOMENTUM_COEF * new))[None])
    returned = average_to_owners(jnp.concatenate(averages))
    for step in (2, 1):
        for p, (order, units) in enumerate(PARTS):
            more = exchange(updates[p], order[step])
            updates[p] = jnp.concatenate([updates[p], more])
    last = [exchange(updates[p], order[0]) for p, (order, _) in enumerate(PARTS)]
    new_weights = apply_updates(base_0, updates, 0, base.shape, None)
    new_momentum = next_momentum(old, returned, momentum.shape)
    new_weights = apply_updates(base_1, last, 1, base.shape, new_weights)
    return new_weights, new_momentum


def solution(mesh):
    finer = Mesh(mesh.devices.reshape(4, 2, 8, 2, 2), EVERY)
    in_specs = (P(R, FSDP, None), P(FSDP, None), P(R, FSDP))
    out_specs = (P(FSDP, None), P(R, FSDP))
    return jax.shard_map(per_device, mesh=finer, in_specs=in_specs, out_specs=out_specs, check_vma=False)
```

time: 111 us -> 90.3 us (0.81)
  the two profiles are of different devices: /device:TPU:1 before, /device:TPU:16 now
where the time goes in v3:
time: 90.3 us; the launch traced here: 90 us
  starting transfers between devices  54.8 us (61%)
  waiting for transfers between devices  24.4 us (27%)
  Pallas kernels  8.89 us (10%)
  between operations  1.13 us (1%)
    ppermute x25, starting transfers between devices, send(): return lax.ppermute(value, EVERY, pairs(there))  54.8 us
    ppermute x25, waiting for transfers between devices, send(): return lax.ppermute(value, EVERY, pairs(there))  24.4 us
    pallas_call x2, Pallas kernels, deltas(): pl.pallas_call(body, in_specs=[pl.BlockSpec(memory_space=pltpu.HBM)] * (2...  5.01 us
    pallas_call x2, Pallas kernels, apply_updates(): pl.pallas_call(body, in_specs=[pl.BlockSpec(memory_space=pltpu.VMEM)] * 4...  3.07 us
  transfers between devices with their start and end apart: 25, of which 9 were waited for; matrix products, arithmetic and copies ran while one was open for 1% of the time, Pallas kernels for 5%

profile of v3, /device:TPU:16, one launch (start us, length us, event | category | flops | bytes accessed | tf_op | source)
XLA Modules:
  0.0 90.0 jit_solution(17179985929049830204)
XLA Ops:
  0.6 2.7 %shard_map.50 = (bf16[4,3,16,896]{3,2,1,0:T(8,128)(2,1)S(1)}, bf16[4,3,16,896]{3,2,1,0:T(8,128)(2,1)S(1)}, bf16[4,2,16,896]{3,2,1,0:T(8,128)(2,1)S(1)}, f32[32,1...) custom-call(bf16[32,28672]{1,0:T(8,128)(2,1)} %bitcast.53, ...), custom_call_target="tpu_custom_call" | custom-call | tf_op jit(solution)/shard_map/pallas_call | solution.py:135
  3.3 0.7 collective-permute-start.3
  4.0 3.1 %collective-permute-start.4 = (bf16[2,32,896]{2,1,0:T(8,128)(2,1)S(1)}, bf16[2,32,896]{2,1,0:T(8,128)(2,1)S(1)}, u32[]{:S(2)}, u32[]{:S(2)}) collective-permute-start(bf16[2,32,896]{2,1,0:T(8,128)(2,1)S(1)} %get-tuple-element.17), channel_id=1, source_target_pairs={{0,2},{1,227},{2,0},{3,225},{4,38},{5,199},{6,36},{7,197},{8,74},{... | collective-permute-start | bytes 344072 | tf_op jit(solution)/shard_map/ppermute | solution.py:42
  7.1 0.4 collective-permute-start.16
  7.5 0.6 collective-permute-start
  8.1 1.1 %collective-permute-start.10 = (bf16[4,3,16,896]{3,2,1,0:T(8,128)(2,1)S(1)}, bf16[4,3,16,896]{3,2,1,0:T(8,128)(2,1)S(1)}, u32[]{:S(2)}, u32[]{:S(2)}) collective-permute-start(bf16[4,3,16,896]{3,2,1,0:T(8,128)(2,1)S(1)} %get-tuple-element.19), channel_id=1, source_target_pairs={{0,64},{1,65},{2,66},{3,67},{4,68},{5,69},{6,70},{7,71},{8,72},{9,... | collective-permute-start | bytes 1032200 | tf_op jit(solution)/shard_map/ppermute | solution.py:42
  9.2 2.4 %shard_map.51 = (bf16[4,3,16,896]{3,2,1,0:T(8,128)(2,1)S(1)}, bf16[4,3,16,896]{3,2,1,0:T(8,128)(2,1)S(1)}, bf16[4,2,16,896]{3,2,1,0:T(8,128)(2,1)S(1)}, f32[32,16,896]{2,1,0:T(8,128)S(1)}) custom-call(bf16[32,28672]{1,0:T(8,128)(2,1)} %bitcast.54, f32[32,28672]{1,0:T(8,128)} %refs_1_.3), custom_call_target="tpu_custom_call" | custom-call | tf_op jit(solution)/shard_map/pallas_call | solution.py:135
  11.6 0.0 collective-permute-done.4
  11.6 13.3 %collective-permute-start.5 = (bf16[2,2,32,896]{3,2,1,0:T(8,128)(2,1)S(1)}, bf16[2,2,32,896]{3,2,1,0:T(8,128)(2,1)S(1)}, u32[]{:S(2)}, u32[]{:S(2)}) collective-permute-start(bf16[2,2,32,896]{3,2,1,0:T(8,128)(2,1)S(1)} %pad_maximum_fusion.2), channel_id=1, source_target_pairs={{0,0},{1,29},{2,2},{3,31},{4,4},{5,25},{6,6},{7,27},{8,8},{9,21},{... | collective-permute-start | bytes 688136 | tf_op jit(solution)/shard_map/ppermute | solution.py:42
  25.0 1.1 %collective-permute-start.17 = (bf16[2,2,16,896]{3,2,1,0:T(8,128)(2,1)S(1)}, bf16[2,2,16,896]{3,2,1,0:T(8,128)(2,1)S(1)}, u32[]{:S(2)}, u32[]{:S(2)}) collective-permute-start(bf16[2,2,16,896]{3,2,1,0:T(8,128)(2,1)S(1)} %add_convert_fusion.2), channel_id=1, source_target_pairs={{0,32},{1,33},{2,34},{3,35},{4,36},{5,37},{6,38},{7,39},{8,40},{9,... | collective-permute-start | bytes 344072 | tf_op jit(solution)/shard_map/ppermute | solution.py:42
  26.0 3.8 %collective-permute-done.5 = bf16[2,2,32,896]{3,2,1,0:T(8,128)(2,1)S(1)} collective-permute-done((bf16[2,2,32,896]{3,2,1,0:T(8,128)(2,1)S(1)}, bf16[2,2,32,896]{3,2,1,0:T(8,128)(2,1)S(1)}, u32[]{:S(2)}, u32[]{:S(2)}) %collective-permute-start.5) | collective-permute-done | bytes 229408 | tf_op jit(solution)/shard_map/ppermute | solution.py:42
  29.8 0.1 collective-permute-start.6
  30.0 0.1 collective-permute-start.18
  30.1 0.0 collective-permute-done
  30.1 2.1 %collective-permute-start.1 = (bf16[2,3,16,896]{3,2,1,0:T(8,128)(2,1)S(1)}, bf16[2,3,16,896]{3,2,1,0:T(8,128)(2,1)S(1)}, u32[]{:S(2)}, u32[]{:S(2)}) collective-permute-start(bf16[2,3,16,896]{3,2,1,0:T(8,128)(2,1)S(1)} %add_convert_fusion.1), channel_id=1, source_target_pairs={{0,64},{1,65},{2,66},{3,67},{4,68},{5,69},{6,70},{7,71},{8,72},{9,... | collective-permute-start | bytes 516104 | tf_op jit(solution)/shard_map/ppermute | solution.py:42
  32.3 2.6 %collective-permute-done.18 = bf16[2,16,896]{2,1,0:T(8,128)(2,1)S(1)} collective-permute-done((bf16[2,16,896]{2,1,0:T(8,128)(2,1)S(1)}, bf16[2,16,896]{2,1,0:T(8,128)(2,1)S(1)}, u32[]{:S(2)}, u32[]{:S(2)}) %collective-permute-start.18) | collective-permute-done | bytes 57376 | tf_op jit(solution)/shard_map/ppermute | solution.py:42
  34.9 0.1 fusion.11
  34.9 0.1 collective-permute-start.19
  35.1 3.5 %collective-permute-start.11 = (bf16[2,3,16,896]{3,2,1,0:T(8,128)(2,1)S(1)}, bf16[2,3,16,896]{3,2,1,0:T(8,128)(2,1)S(1)}, u32[]{:S(2)}, u32[]{:S(2)}) collective-permute-start(bf16[2,3,16,896]{3,2,1,0:T(8,128)(2,1)S(1)} %add_convert_fusion), channel_id=1, source_target_pairs={{0,192},{1,193},{2,194},{3,195},{4,196},{5,197},{6,198},{7,199},{8... | collective-permute-start | bytes 516104 | tf_op jit(solution)/shard_map/ppermute | solution.py:42
  38.6 0.7 collective-permute-done.19
  39.3 4.6 %collective-permute-start.20 = (bf16[2,2,16,896]{3,2,1,0:T(8,128)(2,1)S(1)}, bf16[2,2,16,896]{3,2,1,0:T(8,128)(2,1)S(1)}, u32[]{:S(2)}, u32[]{:S(2)}) collective-permute-start(bf16[2,2,16,896]{3,2,1,0:T(8,128)(2,1)S(1)} %pad_maximum_fusion.9), channel_id=1, source_target_pairs={{0,32},{1,33},{2,34},{3,35},{4,36},{5,37},{6,38},{7,39},{8,40},{9,... | collective-permute-start | bytes 344072 | tf_op jit(solution)/shard_map/ppermute | solution.py:42
  43.9 0.1 collective-permute-start.2
  44.1 1.4 %collective-permute-start.12 = (bf16[3,16,896]{2,1,0:T(8,128)(2,1)S(1)}, bf16[3,16,896]{2,1,0:T(8,128)(2,1)S(1)}, u32[]{:S(2)}, u32[]{:S(2)}) collective-permute-start(bf16[3,16,896]{2,1,0:T(8,128)(2,1)S(1)} %fusion.5), channel_id=1, source_target_pairs={{0,32},{1,33},{2,34},{3,35},{4,36},{5,37},{6,38},{7,39},{8,40},{9,... | collective-permute-start | bytes 258056 | tf_op jit(solution)/shard_map/ppermute | solution.py:42
  45.5 3.0 %collective-permute-done.2 = bf16[3,16,896]{2,1,0:T(8,128)(2,1)S(1)} collective-permute-done((bf16[3,16,896]{2,1,0:T(8,128)(2,1)S(1)}, bf16[3,16,896]{2,1,0:T(8,128)(2,1)S(1)}, u32[]{:S(2)}, u32[]{:S(2)}) %collective-permute-start.2) | collective-permute-done | bytes 86048 | tf_op jit(solution)/shard_map/ppermute | solution.py:42
  48.5 0.1 fusion.9
  48.6 0.1 collective-permute-start.7
  48.7 0.0 collective-permute-done.12
  48.7 0.1 fusion.10
  48.8 1.7 %collective-permute-start.13 = (bf16[1,3,16,896]{3,2,1,0:T(8,128)(2,1)S(1)}, bf16[1,3,16,896]{3,2,1,0:T(8,128)(2,1)S(1)}, u32[]{:S(2)}, u32[]{:S(2)}) collective-permute-start(bf16[1,3,16,896]{3,2,1,0:T(8,128)(2,1)S(1)} %get-tuple-element.27), channel_id=1, source_target_pairs={{0,32},{1,33},{2,34},{3,35},{4,36},{5,37},{6,38},{7,39},{8,40},{9,... | collective-permute-start | bytes 258056 | tf_op jit(solution)/shard_map/ppermute | solution.py:42
  50.6 0.1 collective-permute-start.22
  50.8 0.4 collective-permute-start.21
  51.2 1.9 %collective-permute-done.7 = bf16[1,3,16,896]{3,2,1,0:T(8,128)(2,1)S(1)} collective-permute-done((bf16[1,3,16,896]{3,2,1,0:T(8,128)(2,1)S(1)}, bf16[1,3,16,896]{3,2,1,0:T(8,128)(2,1)S(1)}, u32[]{:S(2)}, u32[]{:S(2)}) %collective-permute-start.7) | collective-permute-done | bytes 86048 | tf_op jit(solution)/shard_map/ppermute | solution.py:42
  53.2 3.3 %collective-permute-start.8 = (bf16[2,3,16,896]{3,2,1,0:T(8,128)(2,1)S(1)}, bf16[2,3,16,896]{3,2,1,0:T(8,128)(2,1)S(1)}, u32[]{:S(2)}, u32[]{:S(2)}) collective-permute-start(bf16[2,3,16,896]{3,2,1,0:T(8,128)(2,1)S(1)} %pad_maximum_fusion.6), channel_id=1, source_target_pairs={{0,64},{1,65},{2,66},{3,67},{4,68},{5,69},{6,70},{7,71},{8,72},{9,... | collective-permute-start | bytes 516104 | tf_op jit(solution)/shard_map/ppermute | solution.py:42
  56.6 0.5 collective-permute-start.14
  57.0 0.0 collective-permute-done.22
  57.0 2.9 %collective-permute-done.8 = bf16[2,3,16,896]{3,2,1,0:T(8,128)(2,1)S(1)} collective-permute-done((bf16[2,3,16,896]{3,2,1,0:T(8,128)(2,1)S(1)}, bf16[2,3,16,896]{3,2,1,0:T(8,128)(2,1)S(1)}, u32[]{:S(2)}, u32[]{:S(2)}) %collective-permute-start.8) | collective-permute-done | bytes 172064 | tf_op jit(solution)/shard_map/ppermute | solution.py:42
  60.0 1.5 %collective-permute-start.9 = (bf16[4,3,16,896]{3,2,1,0:T(8,128)(2,1)S(1)}, bf16[4,3,16,896]{3,2,1,0:T(8,128)(2,1)S(1)}, u32[]{:S(2)}, u32[]{:S(2)}) collective-permute-start(bf16[4,3,16,896]{3,2,1,0:T(8,128)(2,1)S(1)} %pad_maximum_fusion.refs_0_), channel_id=1, source_target_pairs={{0,32},{1,33},{2,34},{3,35},{4,36},{5,37},{6,38},{7,39},{8,40},{9,... | collective-permute-start | bytes 1032200 | tf_op jit(solution)/shard_map/ppermute | solution.py:42
  61.5 1.1 %collective-permute-done.14 = bf16[2,3,16,896]{3,2,1,0:T(8,128)(2,1)S(1)} collective-permute-done((bf16[2,3,16,896]{3,2,1,0:T(8,128)(2,1)S(1)}, bf16[2,3,16,896]{3,2,1,0:T(8,128)(2,1)S(1)}, u32[]{:S(2)}, u32[]{:S(2)}) %collective-permute-start.14) | collective-permute-done | bytes 172064 | tf_op jit(solution)/shard_map/ppermute | solution.py:42
  62.6 4.4 %collective-permute-start.15 = (bf16[4,3,16,896]{3,2,1,0:T(8,128)(2,1)S(1)}, bf16[4,3,16,896]{3,2,1,0:T(8,128)(2,1)S(1)}, u32[]{:S(2)}, u32[]{:S(2)}) collective-permute-start(bf16[4,3,16,896]{3,2,1,0:T(8,128)(2,1)S(1)} %pad_maximum_fusion.1.refs_1_), channel_id=1, source_target_pairs={{0,64},{1,65},{2,66},{3,67},{4,68},{5,69},{6,70},{7,71},{8,72},{9,... | collective-permute-start | bytes 1032200 | tf_op jit(solution)/shard_map/ppermute | solution.py:42
  67.0 6.6 %collective-permute-start.23 = (bf16[2,32,896]{2,1,0:T(8,128)(2,1)S(1)}, bf16[2,32,896]{2,1,0:T(8,128)(2,1)S(1)}, u32[]{:S(2)}, u32[]{:S(2)}) collective-permute-start(bf16[2,32,896]{2,1,0:T(8,128)(2,1)S(1)} %pad_maximum_fusion.10), channel_id=1, source_target_pairs={{0,0},{1,29},{2,2},{3,31},{4,36},{5,57},{6,38},{7,59},{8,72},{9,85... | collective-permute-start | bytes 344072 | tf_op jit(solution)/shard_map/ppermute | solution.py:42
  73.7 3.8 %collective-permute-start.24 = (bf16[2,32,896]{2,1,0:T(8,128)(2,1)S(1)}, bf16[2,32,896]{2,1,0:T(8,128)(2,1)S(1)}, u32[]{:S(2)}, u32[]{:S(2)}) collective-permute-start(bf16[2,32,896]{2,1,0:T(8,128)(2,1)S(1)} %pad_maximum_fusion.11), channel_id=1, source_target_pairs={{0,2},{1,31},{2,0},{3,29},{4,38},{5,59},{6,36},{7,57},{8,74},{9,87... | collective-permute-start | bytes 344072 | tf_op jit(solution)/shard_map/ppermute | solution.py:42
  77.5 0.2 collective-permute-done.23.refs_0_
  77.7 8.2 %collective-permute-done.24.refs_1_ = bf16[2,32,896]{2,1,0:T(8,128)(2,1)S(1)} collective-permute-done((bf16[2,32,896]{2,1,0:T(8,128)(2,1)S(1)}, bf16[2,32,896]{2,1,0:T(8,128)(2,1)S(1)}, u32[]{:S(2)}, u32[]{:S(2)}) %collective-permute-start.24) | collective-permute-done | bytes 114720 | tf_op jit(solution)/shard_map/ppermute | solution.py:42
  85.9 0.8 momentum.1
  86.7 1.5 %shard_map.52.refs_3_ = f32[32,28672]{1,0:T(8,128)} custom-call(f32[32,16,896]{2,1,0:T(8,128)S(1)} %get-tuple-element.22.base_buf, bf16[4,3,16,896]{3,2,1,0:T(8,128)(2,1)S(1)} %pad_maximum_fusion.refs_0_, bf16[4,3,16,896]{3,2,1,0:T(8,128)(2,1)S(1)} %pad_maximum_fusion.1.refs_1_, bf16[4,2,16,896]{3,2,1,0:T(8,128)(2,1)S(1)} %pad_maximum_fusion.4.refs_2_), custom_call_target="tpu_custom_call" | custom-call | tf_op jit(solution)/shard_map/pallas_call | solution.py:162
  88.3 0.0 collective-permute-done.21.refs_2_
  88.3 0.0 collective-permute-done.9.refs_0_
  88.3 1.5 %shard_map.53 = f32[32,28672]{1,0:T(8,128)} custom-call(f32[32,16,896]{2,1,0:T(8,128)S(1)} %get-tuple-element.13.base_buf, bf16[4,3,16,896]{3,2,1,0:T(8,128)(2,1)S(1)} %collective-permute-done.9.refs_0_, bf16[4,3,16,896]{3,2,1,0:T(8,128)(2,1)S(1)} %collective-permute-done.15.refs_1_, ...), custom_call_target="tpu_custom_call", output_to_operand_aliasing={{}: (4, {})} | custom-call | tf_op jit(solution)/shard_map/pallas_call | solution.py:162
  (31 shorter events, 0.6 us)
Async XLA Ops:
  3.3 8.3 %collective-permute-start.3 = (bf16[2,32,896]{2,1,0:T(8,128)(2,1)S(1)}, bf16[2,32,896]{2,1,0:T(8,128)(2,1)S(1)}, u32[]{:S(2)}, u32[]{:S(2)}) collective-permute-start(bf16[2,32,896]{2,1,0:T(8,128)(2,1)S(1)} %get-tuple-element.16), channel_id=1, source_target_pairs={{0,0},{1,225},{2,2},{3,227},{4,36},{5,197},{6,38},{7,199},{8,72},{... | collective-permute-start | bytes 344072 | tf_op jit(solution)/shard_map/ppermute | solution.py:42
  4.0 7.6 %collective-permute-start.4 = (bf16[2,32,896]{2,1,0:T(8,128)(2,1)S(1)}, bf16[2,32,896]{2,1,0:T(8,128)(2,1)S(1)}, u32[]{:S(2)}, u32[]{:S(2)}) collective-permute-start(bf16[2,32,896]{2,1,0:T(8,128)(2,1)S(1)} %get-tuple-element.17), channel_id=1, source_target_pairs={{0,2},{1,227},{2,0},{3,225},{4,38},{5,199},{6,36},{7,197},{8,74},{... | collective-permute-start | bytes 344072 | tf_op jit(solution)/shard_map/ppermute | solution.py:42
  7.1 17.8 %collective-permute-start.16 = (bf16[4,2,16,896]{3,2,1,0:T(8,128)(2,1)S(1)}, bf16[4,2,16,896]{3,2,1,0:T(8,128)(2,1)S(1)}, u32[]{:S(2)}, u32[]{:S(2)}) collective-permute-start(bf16[4,2,16,896]{3,2,1,0:T(8,128)(2,1)S(1)} %get-tuple-element.21), channel_id=1, source_target_pairs={{0,192},{1,193},{2,194},{3,195},{4,196},{5,197},{6,198},{7,199},{8... | collective-permute-start | bytes 688136 | tf_op jit(solution)/shard_map/ppermute | solution.py:42
  7.5 22.6 %collective-permute-start = (bf16[4,3,16,896]{3,2,1,0:T(8,128)(2,1)S(1)}, bf16[4,3,16,896]{3,2,1,0:T(8,128)(2,1)S(1)}, u32[]{:S(2)}, u32[]{:S(2)}) collective-permute-start(bf16[4,3,16,896]{3,2,1,0:T(8,128)(2,1)S(1)} %get-tuple-element.15), channel_id=1, source_target_pairs={{0,32},{1,33},{2,34},{3,35},{4,36},{5,37},{6,38},{7,39},{8,40},{9,... | collective-permute-start | bytes 1032200 | tf_op jit(solution)/shard_map/ppermute | solution.py:42
  8.1 26.9 %collective-permute-start.10 = (bf16[4,3,16,896]{3,2,1,0:T(8,128)(2,1)S(1)}, bf16[4,3,16,896]{3,2,1,0:T(8,128)(2,1)S(1)}, u32[]{:S(2)}, u32[]{:S(2)}) collective-permute-start(bf16[4,3,16,896]{3,2,1,0:T(8,128)(2,1)S(1)} %get-tuple-element.19), channel_id=1, source_target_pairs={{0,64},{1,65},{2,66},{3,67},{4,68},{5,69},{6,70},{7,71},{8,72},{9,... | collective-permute-start | bytes 1032200 | tf_op jit(solution)/shard_map/ppermute | solution.py:42
  11.6 18.2 %collective-permute-start.5 = (bf16[2,2,32,896]{3,2,1,0:T(8,128)(2,1)S(1)}, bf16[2,2,32,896]{3,2,1,0:T(8,128)(2,1)S(1)}, u32[]{:S(2)}, u32[]{:S(2)}) collective-permute-start(bf16[2,2,32,896]{3,2,1,0:T(8,128)(2,1)S(1)} %pad_maximum_fusion.2), channel_id=1, source_target_pairs={{0,0},{1,29},{2,2},{3,31},{4,4},{5,25},{6,6},{7,27},{8,8},{9,21},{... | collective-permute-start | bytes 688136 | tf_op jit(solution)/shard_map/ppermute | solution.py:42
  25.0 5.0 %collective-permute-start.17 = (bf16[2,2,16,896]{3,2,1,0:T(8,128)(2,1)S(1)}, bf16[2,2,16,896]{3,2,1,0:T(8,128)(2,1)S(1)}, u32[]{:S(2)}, u32[]{:S(2)}) collective-permute-start(bf16[2,2,16,896]{3,2,1,0:T(8,128)(2,1)S(1)} %add_convert_fusion.2), channel_id=1, source_target_pairs={{0,32},{1,33},{2,34},{3,35},{4,36},{5,37},{6,38},{7,39},{8,40},{9,... | collective-permute-start | bytes 344072 | tf_op jit(solution)/shard_map/ppermute | solution.py:42
  29.8 2.4 %collective-permute-start.6 = (bf16[2,32,896]{2,1,0:T(8,128)(2,1)S(1)}, bf16[2,32,896]{2,1,0:T(8,128)(2,1)S(1)}, u32[]{:S(2)}, u32[]{:S(2)}) collective-permute-start(bf16[2,32,896]{2,1,0:T(8,128)(2,1)S(1)} %get-tuple-element.33), channel_id=1, source_target_pairs={{0,1},{1,0},{2,3},{3,2},{4,5},{5,4},{6,7},{7,6},{8,9},{9,8},{10,11... | collective-permute-start | bytes 344072 | tf_op jit(solution)/shard_map/ppermute | solution.py:42
  30.0 4.9 %collective-permute-start.18 = (bf16[2,16,896]{2,1,0:T(8,128)(2,1)S(1)}, bf16[2,16,896]{2,1,0:T(8,128)(2,1)S(1)}, u32[]{:S(2)}, u32[]{:S(2)}) collective-permute-start(bf16[2,16,896]{2,1,0:T(8,128)(2,1)S(1)} %fusion.7), channel_id=1, source_target_pairs={{0,64},{1,65},{2,66},{3,67},{4,68},{5,69},{6,70},{7,71},{8,72},{9,... | collective-permute-start | bytes 172040 | tf_op jit(solution)/shard_map/ppermute | solution.py:42
  30.1 13.7 %collective-permute-start.1 = (bf16[2,3,16,896]{3,2,1,0:T(8,128)(2,1)S(1)}, bf16[2,3,16,896]{3,2,1,0:T(8,128)(2,1)S(1)}, u32[]{:S(2)}, u32[]{:S(2)}) collective-permute-start(bf16[2,3,16,896]{3,2,1,0:T(8,128)(2,1)S(1)} %add_convert_fusion.1), channel_id=1, source_target_pairs={{0,64},{1,65},{2,66},{3,67},{4,68},{5,69},{6,70},{7,71},{8,72},{9,... | collective-permute-start | bytes 516104 | tf_op jit(solution)/shard_map/ppermute | solution.py:42
  34.9 4.4 %collective-permute-start.19 = (bf16[1,2,16,896]{3,2,1,0:T(8,128)(2,1)S(1)}, bf16[1,2,16,896]{3,2,1,0:T(8,128)(2,1)S(1)}, u32[]{:S(2)}, u32[]{:S(2)}) collective-permute-start(bf16[1,2,16,896]{3,2,1,0:T(8,128)(2,1)S(1)} %get-tuple-element.29), channel_id=1, source_target_pairs={{0,64},{1,65},{2,66},{3,67},{4,68},{5,69},{6,70},{7,71},{8,72},{9,... | collective-permute-start | bytes 172040 | tf_op jit(solution)/shard_map/ppermute | solution.py:42
  35.1 8.9 %collective-permute-start.11 = (bf16[2,3,16,896]{3,2,1,0:T(8,128)(2,1)S(1)}, bf16[2,3,16,896]{3,2,1,0:T(8,128)(2,1)S(1)}, u32[]{:S(2)}, u32[]{:S(2)}) collective-permute-start(bf16[2,3,16,896]{3,2,1,0:T(8,128)(2,1)S(1)} %add_convert_fusion), channel_id=1, source_target_pairs={{0,192},{1,193},{2,194},{3,195},{4,196},{5,197},{6,198},{7,199},{8... | collective-permute-start | bytes 516104 | tf_op jit(solution)/shard_map/ppermute | solution.py:42
  39.3 11.4 %collective-permute-start.20 = (bf16[2,2,16,896]{3,2,1,0:T(8,128)(2,1)S(1)}, bf16[2,2,16,896]{3,2,1,0:T(8,128)(2,1)S(1)}, u32[]{:S(2)}, u32[]{:S(2)}) collective-permute-start(bf16[2,2,16,896]{3,2,1,0:T(8,128)(2,1)S(1)} %pad_maximum_fusion.9), channel_id=1, source_target_pairs={{0,32},{1,33},{2,34},{3,35},{4,36},{5,37},{6,38},{7,39},{8,40},{9,... | collective-permute-start | bytes 344072 | tf_op jit(solution)/shard_map/ppermute | solution.py:42
  43.9 4.6 %collective-permute-start.2 = (bf16[3,16,896]{2,1,0:T(8,128)(2,1)S(1)}, bf16[3,16,896]{2,1,0:T(8,128)(2,1)S(1)}, u32[]{:S(2)}, u32[]{:S(2)}) collective-permute-start(bf16[3,16,896]{2,1,0:T(8,128)(2,1)S(1)} %fusion.3), channel_id=1, source_target_pairs={{0,192},{1,193},{2,194},{3,195},{4,196},{5,197},{6,198},{7,199},{8... | collective-permute-start | bytes 258056 | tf_op jit(solution)/shard_map/ppermute | solution.py:42
  44.1 4.6 %collective-permute-start.12 = (bf16[3,16,896]{2,1,0:T(8,128)(2,1)S(1)}, bf16[3,16,896]{2,1,0:T(8,128)(2,1)S(1)}, u32[]{:S(2)}, u32[]{:S(2)}) collective-permute-start(bf16[3,16,896]{2,1,0:T(8,128)(2,1)S(1)} %fusion.5), channel_id=1, source_target_pairs={{0,32},{1,33},{2,34},{3,35},{4,36},{5,37},{6,38},{7,39},{8,40},{9,... | collective-permute-start | bytes 258056 | tf_op jit(solution)/shard_map/ppermute | solution.py:42
  48.6 4.6 %collective-permute-start.7 = (bf16[1,3,16,896]{3,2,1,0:T(8,128)(2,1)S(1)}, bf16[1,3,16,896]{3,2,1,0:T(8,128)(2,1)S(1)}, u32[]{:S(2)}, u32[]{:S(2)}) collective-permute-start(bf16[1,3,16,896]{3,2,1,0:T(8,128)(2,1)S(1)} %get-tuple-element.25), channel_id=1, source_target_pairs={{0,192},{1,193},{2,194},{3,195},{4,196},{5,197},{6,198},{7,199},{8... | collective-permute-start | bytes 258056 | tf_op jit(solution)/shard_map/ppermute | solution.py:42
  48.8 7.7 %collective-permute-start.13 = (bf16[1,3,16,896]{3,2,1,0:T(8,128)(2,1)S(1)}, bf16[1,3,16,896]{3,2,1,0:T(8,128)(2,1)S(1)}, u32[]{:S(2)}, u32[]{:S(2)}) collective-permute-start(bf16[1,3,16,896]{3,2,1,0:T(8,128)(2,1)S(1)} %get-tuple-element.27), channel_id=1, source_target_pairs={{0,32},{1,33},{2,34},{3,35},{4,36},{5,37},{6,38},{7,39},{8,40},{9,... | collective-permute-start | bytes 258056 | tf_op jit(solution)/shard_map/ppermute | solution.py:42
  50.6 6.4 %collective-permute-start.22 = (bf16[2,32,896]{2,1,0:T(8,128)(2,1)S(1)}, bf16[2,32,896]{2,1,0:T(8,128)(2,1)S(1)}, u32[]{:S(2)}, u32[]{:S(2)}) collective-permute-start(bf16[2,32,896]{2,1,0:T(8,128)(2,1)S(1)} %bitcast.62), channel_id=1, source_target_pairs={{0,1},{1,0},{2,3},{3,2},{4,5},{5,4},{6,7},{7,6},{8,9},{9,8},{10,11... | collective-permute-start | bytes 344072 | tf_op jit(solution)/shard_map/ppermute | solution.py:42
  50.8 37.5 %collective-permute-start.21 = (bf16[4,2,16,896]{3,2,1,0:T(8,128)(2,1)S(1)}, bf16[4,2,16,896]{3,2,1,0:T(8,128)(2,1)S(1)}, u32[]{:S(2)}, u32[]{:S(2)}) collective-permute-start(bf16[4,2,16,896]{3,2,1,0:T(8,128)(2,1)S(1)} %pad_maximum_fusion.4.refs_2_), channel_id=1, source_target_pairs={{0,192},{1,193},{2,194},{3,195},{4,196},{5,197},{6,198},{7,199},{8... | collective-permute-start | bytes 688136 | tf_op jit(solution)/shard_map/ppermute | solution.py:42
  53.2 6.7 %collective-permute-start.8 = (bf16[2,3,16,896]{3,2,1,0:T(8,128)(2,1)S(1)}, bf16[2,3,16,896]{3,2,1,0:T(8,128)(2,1)S(1)}, u32[]{:S(2)}, u32[]{:S(2)}) collective-permute-start(bf16[2,3,16,896]{3,2,1,0:T(8,128)(2,1)S(1)} %pad_maximum_fusion.6), channel_id=1, source_target_pairs={{0,64},{1,65},{2,66},{3,67},{4,68},{5,69},{6,70},{7,71},{8,72},{9,... | collective-permute-start | bytes 516104 | tf_op jit(solution)/shard_map/ppermute | solution.py:42
  56.6 6.0 %collective-permute-start.14 = (bf16[2,3,16,896]{3,2,1,0:T(8,128)(2,1)S(1)}, bf16[2,3,16,896]{3,2,1,0:T(8,128)(2,1)S(1)}, u32[]{:S(2)}, u32[]{:S(2)}) collective-permute-start(bf16[2,3,16,896]{3,2,1,0:T(8,128)(2,1)S(1)} %pad_maximum_fusion.7), channel_id=1, source_target_pairs={{0,192},{1,193},{2,194},{3,195},{4,196},{5,197},{6,198},{7,199},{8... | collective-permute-start | bytes 516104 | tf_op jit(solution)/shard_map/ppermute | solution.py:42
  60.0 28.3 %collective-permute-start.9 = (bf16[4,3,16,896]{3,2,1,0:T(8,128)(2,1)S(1)}, bf16[4,3,16,896]{3,2,1,0:T(8,128)(2,1)S(1)}, u32[]{:S(2)}, u32[]{:S(2)}) collective-permute-start(bf16[4,3,16,896]{3,2,1,0:T(8,128)(2,1)S(1)} %pad_maximum_fusion.refs_0_), channel_id=1, source_target_pairs={{0,32},{1,33},{2,34},{3,35},{4,36},{5,37},{6,38},{7,39},{8,40},{9,... | collective-permute-start | bytes 1032200 | tf_op jit(solution)/shard_map/ppermute | solution.py:42
  62.6 25.7 %collective-permute-start.15 = (bf16[4,3,16,896]{3,2,1,0:T(8,128)(2,1)S(1)}, bf16[4,3,16,896]{3,2,1,0:T(8,128)(2,1)S(1)}, u32[]{:S(2)}, u32[]{:S(2)}) collective-permute-start(bf16[4,3,16,896]{3,2,1,0:T(8,128)(2,1)S(1)} %pad_maximum_fusion.1.refs_1_), channel_id=1, source_target_pairs={{0,64},{1,65},{2,66},{3,67},{4,68},{5,69},{6,70},{7,71},{8,72},{9,... | collective-permute-start | bytes 1032200 | tf_op jit(solution)/shard_map/ppermute | solution.py:42
  67.0 10.7 %collective-permute-start.23 = (bf16[2,32,896]{2,1,0:T(8,128)(2,1)S(1)}, bf16[2,32,896]{2,1,0:T(8,128)(2,1)S(1)}, u32[]{:S(2)}, u32[]{:S(2)}) collective-permute-start(bf16[2,32,896]{2,1,0:T(8,128)(2,1)S(1)} %pad_maximum_fusion.10), channel_id=1, source_target_pairs={{0,0},{1,29},{2,2},{3,31},{4,36},{5,57},{6,38},{7,59},{8,72},{9,85... | collective-permute-start | bytes 344072 | tf_op jit(solution)/shard_map/ppermute | solution.py:42
  73.7 12.2 %collective-permute-start.24 = (bf16[2,32,896]{2,1,0:T(8,128)(2,1)S(1)}, bf16[2,32,896]{2,1,0:T(8,128)(2,1)S(1)}, u32[]{:S(2)}, u32[]{:S(2)}) collective-permute-start(bf16[2,32,896]{2,1,0:T(8,128)(2,1)S(1)} %pad_maximum_fusion.11), channel_id=1, source_target_pairs={{0,2},{1,31},{2,0},{3,29},{4,38},{5,59},{6,36},{7,57},{8,74},{9,87... | collective-permute-start | bytes 344072 | tf_op jit(solution)/shard_map/ppermute | solution.py:42

commit v4 on v3

--- a/solution.py
+++ b/solution.py
@@ -21,7 +21,7 @@
 
 
 def column_plane(r, z, c):
-    return r ^ z ^ (7 * c)
+    return r ^ z ^ (5 * c)
 
 
 def device(r, z, xh, c):
@@ -67,8 +67,7 @@
 def place_of(peer_index, unit):
     r = lax.axis_index(R) ^ peer_index
     z, xh, c = lax.axis_index("z"), lax.axis_index("xh"), lax.axis_index("c")
-    core = c ^ (unit // 4)
-    column = 4 * column_plane(r, z, core) + 2 * (xh ^ (unit // 2 % 2)) + core
+    column = 4 * column_plane(r, z, c) + 2 * (xh ^ (unit // 4)) + (c ^ (unit // 2 % 2))
     return HALF * (unit % 2), pl.multiple_of(column * WIDE, 128)
 
 
@@ -118,7 +117,7 @@
         if lead:
             for dx, dc, copy in old_copies:
                 copy.wait()
-                moved[dx][dc] = old_buf[dx, dc].astype(jnp.bfloat16)
+                moved[dc][dx] = old_buf[dx, dc].astype(jnp.bfloat16)
 
     more = [momentum] if lead else []
     out_shape = [pltpu.VMEM(shape, jnp.bfloat16) for shape in shapes_of()]
@@ -177,14 +176,14 @@
 def next_momentum(old, returned, shape):
     rows = 2 * HALF
 
-    def body(old_buf, *refs):
-        pieces, out_hbm, out_buf, out_sem = refs[:2], refs[2], refs[3], refs[4]
+    def body(old_buf, stayed, came, out_hbm, out_buf, out_sem):
         xh, c = lax.axis_index("xh"), lax.axis_index("c")
         copies = []
         for dx in range(2):
             for dc in range(2):
                 row = pl.multiple_of(rows * (2 * (xh ^ dx) + (c ^ dc)), rows)
-                out_buf[dx, dc] = MOMENTUM_COEF * old_buf[dx, dc] + pieces[dx][dc].astype(jnp.float32)
+                average = came[dx] if dc else stayed[dx, 0]
+                out_buf[dx, dc] = MOMENTUM_COEF * old_buf[dx, dc] + average.astype(jnp.float32)
                 copy = pltpu.make_async_copy(
                     out_buf.at[dx, dc], out_hbm.at[pl.ds(row, rows)], out_sem.at[dx, dc]
                 )
@@ -204,25 +203,27 @@
     )(in_vmem(old), *[in_vmem(v) for v in returned])
 
 
-def momentum_to_holders(m):
+def momentum_to_holders(stays, leaves):
     holder = {(column_plane(r, z, c), z, c): r for r in range(8) for z in range(8) for c in range(2)}
-    moved = [send(m[dx], lambda r, z, xh, c: (holder[z, r, c], z, xh ^ dx, c)) for dx in range(2)]
     owner = {(r, column_plane(r, z, c), c): z for r in range(8) for z in range(8) for c in range(2)}
-    m = send(jnp.stack(moved), lambda r, z, xh, c: (r, owner[r, z, c], xh, c))
-    other = send(m[:, 1], lambda r, z, xh, c: (r, z, xh, 1 - c))
-    return jnp.stack([m[:, 0], other]).reshape(8, HALF, WIDE)
-
-
-def average_to_owners(average):
-    average = average.reshape(2, 2, 2 * HALF, WIDE)
-    other = send(average[1], lambda r, z, xh, c: (r, z, xh, 1 - c))
-    return [
+    other = send(leaves, lambda r, z, xh, c: (r, z, xh, 1 - c))
+    moved = [
         send(
-            jnp.stack([average[0, dx], other[dx]]),
-            lambda r, z, xh, c: (z, column_plane(r, z, c), xh ^ dx, c),
+            jnp.stack([stays[dx], other[dx]]), lambda r, z, xh, c: (holder[z, r, c], z, xh ^ dx, c)
         )
         for dx in range(2)
     ]
+    m = send(jnp.stack(moved), lambda r, z, xh, c: (r, owner[r, z, c], xh, c))
+    return m.reshape(8, HALF, WIDE)
+
+
+def average_to_owners(average):
+    average = average.reshape(2, 2, 2 * HALF, WIDE)
+    other = send(average[1], lambda r, z, xh, c: (r, z, 1 - xh, c))
+    average = jnp.stack([average[0], other])
+    average = send(average, lambda r, z, xh, c: (z, column_plane(r, z, c), xh, c))
+    other = send(average[:, 1], lambda r, z, xh, c: (r, z, xh, 1 - c))
+    return average, other
 
 
 def f32(value):
@@ -239,8 +240,8 @@
 
 def outer_step(local, base, momentum):
     count = lax.axis_size(R)
-    *sends, base_1, m_0, m_1, old = deltas(local, base, momentum, 1)
-    held = momentum_to_holders([m_0, m_1])
+    *sends, base_1, stays, leaves, old = deltas(local, base, momentum, 1)
+    held = momentum_to_holders(stays, leaves)
     first = [exchange(sends[p], order[0]) for p, (order, _) in enumerate(PARTS)]
     *kept, base_0 = deltas(local, base, None, 0)
     second, third, averages, updates = [], [], [], []

time: 90.3 us -> 79.3 us (0.88)
  the two profiles are of different devices: /device:TPU:16 before, /device:TPU:163 now
where the time goes in v4:
time: 79.3 us; the launch traced here: 79 us
  starting transfers between devices  48.3 us (61%)
  waiting for transfers between devices  19.9 us (25%)
  Pallas kernels  8.88 us (11%)
  between operations  1.08 us (1%)
    ppermute x25, starting transfers between devices, send(): return lax.ppermute(value, EVERY, pairs(there))  48.3 us
    ppermute x25, waiting for transfers between devices, send(): return lax.ppermute(value, EVERY, pairs(there))  19.9 us
    pallas_call x2, Pallas kernels, deltas(): pl.pallas_call(body, in_specs=[pl.BlockSpec(memory_space=pltpu.HBM)] * (2...  5.01 us
    pallas_call x2, Pallas kernels, apply_updates(): pl.pallas_call(body, in_specs=[pl.BlockSpec(memory_space=pltpu.VMEM)] * 4...  3.05 us
  transfers between devices with their start and end apart: 25, of which 10 were waited for; matrix products, arithmetic and copies ran while one was open for 1% of the time, Pallas kernels for 6%

profile of v4, /device:TPU:163, one launch (start us, length us, event | category | flops | bytes accessed | tf_op | source)
XLA Modules:
  0.0 79.0 jit_solution(6895208091516857944)
XLA Ops:
  0.6 2.6 %shard_map.50 = (bf16[4,3,16,896]{3,2,1,0:T(8,128)(2,1)S(1)}, bf16[4,3,16,896]{3,2,1,0:T(8,128)(2,1)S(1)}, bf16[4,2,16,896]{3,2,1,0:T(8,128)(2,1)S(1)}, f32[32,1...) custom-call(bf16[32,28672]{1,0:T(8,128)(2,1)} %bitcast.45, ...), custom_call_target="tpu_custom_call" | custom-call | tf_op jit(solution)/shard_map/pallas_call | solution.py:134
  3.3 0.8 collective-permute-start.3
  4.0 2.7 %collective-permute-start.16 = (bf16[4,2,16,896]{3,2,1,0:T(8,128)(2,1)S(1)}, bf16[4,2,16,896]{3,2,1,0:T(8,128)(2,1)S(1)}, u32[]{:S(2)}, u32[]{:S(2)}) collective-permute-start(bf16[4,2,16,896]{3,2,1,0:T(8,128)(2,1)S(1)} %get-tuple-element.21), channel_id=1, source_target_pairs={{0,192},{1,193},{2,194},{3,195},{4,196},{5,197},{6,198},{7,199},{8... | collective-permute-start | bytes 688136 | tf_op jit(solution)/shard_map/ppermute | solution.py:42
  6.8 0.3 collective-permute-start
  7.0 2.4 %shard_map.51 = (bf16[4,3,16,896]{3,2,1,0:T(8,128)(2,1)S(1)}, bf16[4,3,16,896]{3,2,1,0:T(8,128)(2,1)S(1)}, bf16[4,2,16,896]{3,2,1,0:T(8,128)(2,1)S(1)}, f32[32,16,896]{2,1,0:T(8,128)S(1)}) custom-call(bf16[32,28672]{1,0:T(8,128)(2,1)} %bitcast.46, f32[32,28672]{1,0:T(8,128)} %refs_1_.3), custom_call_target="tpu_custom_call" | custom-call | tf_op jit(solution)/shard_map/pallas_call | solution.py:134
  9.5 2.2 %collective-permute-start.5 = (bf16[2,32,896]{2,1,0:T(8,128)(2,1)S(1)}, bf16[2,32,896]{2,1,0:T(8,128)(2,1)S(1)}, u32[]{:S(2)}, u32[]{:S(2)}) collective-permute-start(bf16[2,32,896]{2,1,0:T(8,128)(2,1)S(1)} %pad_maximum_fusion.10), channel_id=1, source_target_pairs={{0,2},{1,163},{2,0},{3,161},{4,38},{5,135},{6,36},{7,133},{8,74},{... | collective-permute-start | bytes 344072 | tf_op jit(solution)/shard_map/ppermute | solution.py:42
  11.7 0.7 collective-permute-start.4
  12.4 0.0 collective-permute-done.16
  12.5 1.6 %collective-permute-start.17 = (bf16[2,2,16,896]{3,2,1,0:T(8,128)(2,1)S(1)}, bf16[2,2,16,896]{3,2,1,0:T(8,128)(2,1)S(1)}, u32[]{:S(2)}, u32[]{:S(2)}) collective-permute-start(bf16[2,2,16,896]{3,2,1,0:T(8,128)(2,1)S(1)} %add_convert_fusion.2), channel_id=1, source_target_pairs={{0,32},{1,33},{2,34},{3,35},{4,36},{5,37},{6,38},{7,39},{8,40},{9,... | collective-permute-start | bytes 344072 | tf_op jit(solution)/shard_map/ppermute | solution.py:42
  14.1 4.7 %collective-permute-done.5 = bf16[2,32,896]{2,1,0:T(8,128)(2,1)S(1)} collective-permute-done((bf16[2,32,896]{2,1,0:T(8,128)(2,1)S(1)}, bf16[2,32,896]{2,1,0:T(8,128)(2,1)S(1)}, u32[]{:S(2)}, u32[]{:S(2)}) %collective-permute-start.5) | collective-permute-done | bytes 114720 | tf_op jit(solution)/shard_map/ppermute | solution.py:42
  18.7 0.0 collective-permute-done.4
  18.8 2.6 %collective-permute-start.6 = (bf16[2,2,32,896]{3,2,1,0:T(8,128)(2,1)S(1)}, bf16[2,2,32,896]{3,2,1,0:T(8,128)(2,1)S(1)}, u32[]{:S(2)}, u32[]{:S(2)}) collective-permute-start(bf16[2,2,32,896]{3,2,1,0:T(8,128)(2,1)S(1)} %pad_maximum_fusion.2), channel_id=1, source_target_pairs={{0,0},{1,21},{2,2},{3,23},{4,4},{5,17},{6,6},{7,19},{8,8},{9,29},{... | collective-permute-start | bytes 688136 | tf_op jit(solution)/shard_map/ppermute | solution.py:42
  21.3 0.0 collective-permute-done.17
  21.4 0.2 collective-permute-start.18
  21.7 1.4 %collective-permute-start.1 = (bf16[2,3,16,896]{3,2,1,0:T(8,128)(2,1)S(1)}, bf16[2,3,16,896]{3,2,1,0:T(8,128)(2,1)S(1)}, u32[]{:S(2)}, u32[]{:S(2)}) collective-permute-start(bf16[2,3,16,896]{3,2,1,0:T(8,128)(2,1)S(1)} %add_convert_fusion.1), channel_id=1, source_target_pairs={{0,64},{1,65},{2,66},{3,67},{4,68},{5,69},{6,70},{7,71},{8,72},{9,... | collective-permute-start | bytes 516104 | tf_op jit(solution)/shard_map/ppermute | solution.py:42
  23.1 1.4 %collective-permute-done.18 = bf16[2,16,896]{2,1,0:T(8,128)(2,1)S(1)} collective-permute-done((bf16[2,16,896]{2,1,0:T(8,128)(2,1)S(1)}, bf16[2,16,896]{2,1,0:T(8,128)(2,1)S(1)}, u32[]{:S(2)}, u32[]{:S(2)}) %collective-permute-start.18) | collective-permute-done | bytes 57376 | tf_op jit(solution)/shard_map/ppermute | solution.py:42
  24.5 5.0 %collective-permute-done.6 = bf16[2,2,32,896]{3,2,1,0:T(8,128)(2,1)S(1)} collective-permute-done((bf16[2,2,32,896]{3,2,1,0:T(8,128)(2,1)S(1)}, bf16[2,2,32,896]{3,2,1,0:T(8,128)(2,1)S(1)}, u32[]{:S(2)}, u32[]{:S(2)}) %collective-permute-start.6) | collective-permute-done | bytes 229408 | tf_op jit(solution)/shard_map/ppermute | solution.py:42
  29.6 0.1 fusion.11
  29.6 0.9 %collective-permute-start.19 = (bf16[1,2,16,896]{3,2,1,0:T(8,128)(2,1)S(1)}, bf16[1,2,16,896]{3,2,1,0:T(8,128)(2,1)S(1)}, u32[]{:S(2)}, u32[]{:S(2)}) collective-permute-start(bf16[1,2,16,896]{3,2,1,0:T(8,128)(2,1)S(1)} %get-tuple-element.29), channel_id=1, source_target_pairs={{0,64},{1,65},{2,66},{3,67},{4,68},{5,69},{6,70},{7,71},{8,72},{9,... | collective-permute-start | bytes 172040 | tf_op jit(solution)/shard_map/ppermute | solution.py:42
  30.5 0.0 collective-permute-done.10
  30.6 0.1 collective-permute-start.11
  30.7 2.1 %collective-permute-done.19 = bf16[1,2,16,896]{3,2,1,0:T(8,128)(2,1)S(1)} collective-permute-done((bf16[1,2,16,896]{3,2,1,0:T(8,128)(2,1)S(1)}, bf16[1,2,16,896]{3,2,1,0:T(8,128)(2,1)S(1)}, u32[]{:S(2)}, u32[]{:S(2)}) %collective-permute-start.19) | collective-permute-done | bytes 57376 | tf_op jit(solution)/shard_map/ppermute | solution.py:42
  32.8 1.6 %collective-permute-start.20 = (bf16[2,2,16,896]{3,2,1,0:T(8,128)(2,1)S(1)}, bf16[2,2,16,896]{3,2,1,0:T(8,128)(2,1)S(1)}, u32[]{:S(2)}, u32[]{:S(2)}) collective-permute-start(bf16[2,2,16,896]{3,2,1,0:T(8,128)(2,1)S(1)} %pad_maximum_fusion.11), channel_id=1, source_target_pairs={{0,32},{1,33},{2,34},{3,35},{4,36},{5,37},{6,38},{7,39},{8,40},{9,... | collective-permute-start | bytes 344072 | tf_op jit(solution)/shard_map/ppermute | solution.py:42
  34.4 1.3 %collective-permute-start.2 = (bf16[3,16,896]{2,1,0:T(8,128)(2,1)S(1)}, bf16[3,16,896]{2,1,0:T(8,128)(2,1)S(1)}, u32[]{:S(2)}, u32[]{:S(2)}) collective-permute-start(bf16[3,16,896]{2,1,0:T(8,128)(2,1)S(1)} %fusion.3), channel_id=1, source_target_pairs={{0,192},{1,193},{2,194},{3,195},{4,196},{5,197},{6,198},{7,199},{8... | collective-permute-start | bytes 258056 | tf_op jit(solution)/shard_map/ppermute | solution.py:42
  35.7 0.4 collective-permute-done.11
  36.2 2.3 %collective-permute-start.12 = (bf16[3,16,896]{2,1,0:T(8,128)(2,1)S(1)}, bf16[3,16,896]{2,1,0:T(8,128)(2,1)S(1)}, u32[]{:S(2)}, u32[]{:S(2)}) collective-permute-start(bf16[3,16,896]{2,1,0:T(8,128)(2,1)S(1)} %fusion.5), channel_id=1, source_target_pairs={{0,32},{1,33},{2,34},{3,35},{4,36},{5,37},{6,38},{7,39},{8,40},{9,... | collective-permute-start | bytes 258056 | tf_op jit(solution)/shard_map/ppermute | solution.py:42
  38.4 0.6 collective-permute-done.2
  39.0 0.1 fusion.9
  39.1 1.3 %collective-permute-start.7 = (bf16[1,3,16,896]{3,2,1,0:T(8,128)(2,1)S(1)}, bf16[1,3,16,896]{3,2,1,0:T(8,128)(2,1)S(1)}, u32[]{:S(2)}, u32[]{:S(2)}) collective-permute-start(bf16[1,3,16,896]{3,2,1,0:T(8,128)(2,1)S(1)} %get-tuple-element.25), channel_id=1, source_target_pairs={{0,192},{1,193},{2,194},{3,195},{4,196},{5,197},{6,198},{7,199},{8... | collective-permute-start | bytes 258056 | tf_op jit(solution)/shard_map/ppermute | solution.py:42
  40.5 0.1 collective-permute-done.12
  40.6 0.1 fusion.10
  40.7 1.5 %collective-permute-start.13 = (bf16[1,3,16,896]{3,2,1,0:T(8,128)(2,1)S(1)}, bf16[1,3,16,896]{3,2,1,0:T(8,128)(2,1)S(1)}, u32[]{:S(2)}, u32[]{:S(2)}) collective-permute-start(bf16[1,3,16,896]{3,2,1,0:T(8,128)(2,1)S(1)} %get-tuple-element.27), channel_id=1, source_target_pairs={{0,32},{1,33},{2,34},{3,35},{4,36},{5,37},{6,38},{7,39},{8,40},{9,... | collective-permute-start | bytes 258056 | tf_op jit(solution)/shard_map/ppermute | solution.py:42
  42.3 0.1 collective-permute-start.22
  42.4 0.0 collective-permute-done.20
  42.4 1.0 %collective-permute-start.21 = (bf16[4,2,16,896]{3,2,1,0:T(8,128)(2,1)S(1)}, bf16[4,2,16,896]{3,2,1,0:T(8,128)(2,1)S(1)}, u32[]{:S(2)}, u32[]{:S(2)}) collective-permute-start(bf16[4,2,16,896]{3,2,1,0:T(8,128)(2,1)S(1)} %pad_maximum_fusion.3.refs_2_), channel_id=1, source_target_pairs={{0,192},{1,193},{2,194},{3,195},{4,196},{5,197},{6,198},{7,199},{8... | collective-permute-start | bytes 688136 | tf_op jit(solution)/shard_map/ppermute | solution.py:42
  43.4 0.4 collective-permute-done.7
  43.8 0.3 collective-permute-start.8
  44.1 0.0 collective-permute-done.13
  44.1 2.5 %collective-permute-start.14 = (bf16[2,3,16,896]{3,2,1,0:T(8,128)(2,1)S(1)}, bf16[2,3,16,896]{3,2,1,0:T(8,128)(2,1)S(1)}, u32[]{:S(2)}, u32[]{:S(2)}) collective-permute-start(bf16[2,3,16,896]{3,2,1,0:T(8,128)(2,1)S(1)} %pad_maximum_fusion.6), channel_id=1, source_target_pairs={{0,192},{1,193},{2,194},{3,195},{4,196},{5,197},{6,198},{7,199},{8... | collective-permute-start | bytes 516104 | tf_op jit(solution)/shard_map/ppermute | solution.py:42
  46.7 1.8 %collective-permute-done.22 = bf16[2,32,896]{2,1,0:T(8,128)(2,1)S(1)} collective-permute-done((bf16[2,32,896]{2,1,0:T(8,128)(2,1)S(1)}, bf16[2,32,896]{2,1,0:T(8,128)(2,1)S(1)}, u32[]{:S(2)}, u32[]{:S(2)}) %collective-permute-start.22) | collective-permute-done | bytes 114720 | tf_op jit(solution)/shard_map/ppermute | solution.py:42
  48.5 4.2 %collective-permute-start.23 = (bf16[2,2,32,896]{3,2,0,1:T(8,128)(2,1)S(1)}, bf16[2,2,32,896]{3,2,0,1:T(8,128)(2,1)S(1)}, u32[]{:S(2)}, u32[]{:S(2)}) collective-permute-start(bf16[2,2,32,896]{3,2,0,1:T(8,128)(2,1)S(1)} %pad_maximum_fusion.4), channel_id=1, source_target_pairs={{0,0},{1,21},{2,2},{3,23},{4,36},{5,49},{6,38},{7,51},{8,72},{9,93... | collective-permute-start | bytes 688136 | tf_op jit(solution)/shard_map/ppermute | solution.py:42
  52.7 0.1 collective-permute-start.9
  52.9 3.0 %collective-permute-start.15 = (bf16[4,3,16,896]{3,2,1,0:T(8,128)(2,1)S(1)}, bf16[4,3,16,896]{3,2,1,0:T(8,128)(2,1)S(1)}, u32[]{:S(2)}, u32[]{:S(2)}) collective-permute-start(bf16[4,3,16,896]{3,2,1,0:T(8,128)(2,1)S(1)} %pad_maximum_fusion.1.refs_1_), channel_id=1, source_target_pairs={{0,64},{1,65},{2,66},{3,67},{4,68},{5,69},{6,70},{7,71},{8,72},{9,... | collective-permute-start | bytes 1032200 | tf_op jit(solution)/shard_map/ppermute | solution.py:42
  55.9 3.3 %collective-permute-done.23 = bf16[2,2,32,896]{3,2,0,1:T(8,128)(2,1)S(1)} collective-permute-done((bf16[2,2,32,896]{3,2,0,1:T(8,128)(2,1)S(1)}, bf16[2,2,32,896]{3,2,0,1:T(8,128)(2,1)S(1)}, u32[]{:S(2)}, u32[]{:S(2)}) %collective-permute-start.23) | collective-permute-done | bytes 229408 | tf_op jit(solution)/shard_map/ppermute | solution.py:42
  59.2 15.7 %collective-permute-start.24 = (bf16[2,32,896]{2,1,0:T(8,128)(2,1)S(1)}, bf16[2,32,896]{2,1,0:T(8,128)(2,1)S(1)}, u32[]{:S(2)}, u32[]{:S(2)}) collective-permute-start(bf16[2,32,896]{2,1,0:T(8,128)(2,1)S(1)} %slice_bitcast_fusion), channel_id=1, source_target_pairs={{0,1},{1,0},{2,3},{3,2},{4,5},{5,4},{6,7},{7,6},{8,9},{9,8},{10,11... | collective-permute-start | bytes 344072 | tf_op jit(solution)/shard_map/ppermute | solution.py:42
  74.9 1.5 %shard_map.52.refs_3_ = f32[32,28672]{1,0:T(8,128)} custom-call(f32[32,16,896]{2,1,0:T(8,128)S(1)} %get-tuple-element.22.base_buf, bf16[4,3,16,896]{3,2,1,0:T(8,128)(2,1)S(1)} %pad_maximum_fusion.refs_0_, bf16[4,3,16,896]{3,2,1,0:T(8,128)(2,1)S(1)} %pad_maximum_fusion.1.refs_1_, bf16[4,2,16,896]{3,2,1,0:T(8,128)(2,1)S(1)} %pad_maximum_fusion.3.refs_2_), custom_call_target="tpu_custom_call" | custom-call | tf_op jit(solution)/shard_map/pallas_call | solution.py:161
  76.5 0.8 %momentum.1 = f32[128,896]{1,0:T(8,128)} custom-call(f32[2,2,32,896]{3,2,1,0:T(8,128)S(1)} %get-tuple-element.23.old_buf, bf16[2,2,32,896]{3,2,1,0:T(8,128)(2,1)S(1)} %copy.6.stayed, bf16[2,32,896]{2,1,0:T(8,128)(2,1)S(1)} %collective-permute-done.24.came), custom_call_target="tpu_custom_call" | custom-call | tf_op jit(solution)/shard_map/momentum/pallas_call | solution.py:195
  77.3 1.5 %shard_map.53 = f32[32,28672]{1,0:T(8,128)} custom-call(f32[32,16,896]{2,1,0:T(8,128)S(1)} %get-tuple-element.13.base_buf, bf16[4,3,16,896]{3,2,1,0:T(8,128)(2,1)S(1)} %collective-permute-done.9.refs_0_, bf16[4,3,16,896]{3,2,1,0:T(8,128)(2,1)S(1)} %collective-permute-done.15.refs_1_, ...), custom_call_target="tpu_custom_call", output_to_operand_aliasing={{}: (4, {})} | custom-call | tf_op jit(solution)/shard_map/pallas_call | solution.py:161
  (31 shorter events, 0.6 us)
Async XLA Ops:
  3.3 6.1 %collective-permute-start.3 = (bf16[2,32,896]{2,1,0:T(8,128)(2,1)S(1)}, bf16[2,32,896]{2,1,0:T(8,128)(2,1)S(1)}, u32[]{:S(2)}, u32[]{:S(2)}) collective-permute-start(bf16[2,32,896]{2,1,0:T(8,128)(2,1)S(1)} %get-tuple-element.17), channel_id=1, source_target_pairs={{0,1},{1,0},{2,3},{3,2},{4,5},{5,4},{6,7},{7,6},{8,9},{9,8},{10,11... | collective-permute-start | bytes 344072 | tf_op jit(solution)/shard_map/ppermute | solution.py:42
  4.0 8.4 %collective-permute-start.16 = (bf16[4,2,16,896]{3,2,1,0:T(8,128)(2,1)S(1)}, bf16[4,2,16,896]{3,2,1,0:T(8,128)(2,1)S(1)}, u32[]{:S(2)}, u32[]{:S(2)}) collective-permute-start(bf16[4,2,16,896]{3,2,1,0:T(8,128)(2,1)S(1)} %get-tuple-element.21), channel_id=1, source_target_pairs={{0,192},{1,193},{2,194},{3,195},{4,196},{5,197},{6,198},{7,199},{8... | collective-permute-start | bytes 688136 | tf_op jit(solution)/shard_map/ppermute | solution.py:42
  6.8 14.8 %collective-permute-start = (bf16[4,3,16,896]{3,2,1,0:T(8,128)(2,1)S(1)}, bf16[4,3,16,896]{3,2,1,0:T(8,128)(2,1)S(1)}, u32[]{:S(2)}, u32[]{:S(2)}) collective-permute-start(bf16[4,3,16,896]{3,2,1,0:T(8,128)(2,1)S(1)} %get-tuple-element.15), channel_id=1, source_target_pairs={{0,32},{1,33},{2,34},{3,35},{4,36},{5,37},{6,38},{7,39},{8,40},{9,... | collective-permute-start | bytes 1032200 | tf_op jit(solution)/shard_map/ppermute | solution.py:42
  7.0 23.5 %collective-permute-start.10 = (bf16[4,3,16,896]{3,2,1,0:T(8,128)(2,1)S(1)}, bf16[4,3,16,896]{3,2,1,0:T(8,128)(2,1)S(1)}, u32[]{:S(2)}, u32[]{:S(2)}) collective-permute-start(bf16[4,3,16,896]{3,2,1,0:T(8,128)(2,1)S(1)} %get-tuple-element.19), channel_id=1, source_target_pairs={{0,64},{1,65},{2,66},{3,67},{4,68},{5,69},{6,70},{7,71},{8,72},{9,... | collective-permute-start | bytes 1032200 | tf_op jit(solution)/shard_map/ppermute | solution.py:42
  9.5 9.2 %collective-permute-start.5 = (bf16[2,32,896]{2,1,0:T(8,128)(2,1)S(1)}, bf16[2,32,896]{2,1,0:T(8,128)(2,1)S(1)}, u32[]{:S(2)}, u32[]{:S(2)}) collective-permute-start(bf16[2,32,896]{2,1,0:T(8,128)(2,1)S(1)} %pad_maximum_fusion.10), channel_id=1, source_target_pairs={{0,2},{1,163},{2,0},{3,161},{4,38},{5,135},{6,36},{7,133},{8,74},{... | collective-permute-start | bytes 344072 | tf_op jit(solution)/shard_map/ppermute | solution.py:42
  11.7 7.0 %collective-permute-start.4 = (bf16[2,32,896]{2,1,0:T(8,128)(2,1)S(1)}, bf16[2,32,896]{2,1,0:T(8,128)(2,1)S(1)}, u32[]{:S(2)}, u32[]{:S(2)}) collective-permute-start(bf16[2,32,896]{2,1,0:T(8,128)(2,1)S(1)} %pad_maximum_fusion.9), channel_id=1, source_target_pairs={{0,0},{1,161},{2,2},{3,163},{4,36},{5,133},{6,38},{7,135},{8,72},{... | collective-permute-start | bytes 344072 | tf_op jit(solution)/shard_map/ppermute | solution.py:42
  12.5 8.9 %collective-permute-start.17 = (bf16[2,2,16,896]{3,2,1,0:T(8,128)(2,1)S(1)}, bf16[2,2,16,896]{3,2,1,0:T(8,128)(2,1)S(1)}, u32[]{:S(2)}, u32[]{:S(2)}) collective-permute-start(bf16[2,2,16,896]{3,2,1,0:T(8,128)(2,1)S(1)} %add_convert_fusion.2), channel_id=1, source_target_pairs={{0,32},{1,33},{2,34},{3,35},{4,36},{5,37},{6,38},{7,39},{8,40},{9,... | collective-permute-start | bytes 344072 | tf_op jit(solution)/shard_map/ppermute | solution.py:42
  18.8 10.8 %collective-permute-start.6 = (bf16[2,2,32,896]{3,2,1,0:T(8,128)(2,1)S(1)}, bf16[2,2,32,896]{3,2,1,0:T(8,128)(2,1)S(1)}, u32[]{:S(2)}, u32[]{:S(2)}) collective-permute-start(bf16[2,2,32,896]{3,2,1,0:T(8,128)(2,1)S(1)} %pad_maximum_fusion.2), channel_id=1, source_target_pairs={{0,0},{1,21},{2,2},{3,23},{4,4},{5,17},{6,6},{7,19},{8,8},{9,29},{... | collective-permute-start | bytes 688136 | tf_op jit(solution)/shard_map/ppermute | solution.py:42
  21.4 3.1 %collective-permute-start.18 = (bf16[2,16,896]{2,1,0:T(8,128)(2,1)S(1)}, bf16[2,16,896]{2,1,0:T(8,128)(2,1)S(1)}, u32[]{:S(2)}, u32[]{:S(2)}) collective-permute-start(bf16[2,16,896]{2,1,0:T(8,128)(2,1)S(1)} %fusion.7), channel_id=1, source_target_pairs={{0,64},{1,65},{2,66},{3,67},{4,68},{5,69},{6,70},{7,71},{8,72},{9,... | collective-permute-start | bytes 172040 | tf_op jit(solution)/shard_map/ppermute | solution.py:42
  21.7 12.7 %collective-permute-start.1 = (bf16[2,3,16,896]{3,2,1,0:T(8,128)(2,1)S(1)}, bf16[2,3,16,896]{3,2,1,0:T(8,128)(2,1)S(1)}, u32[]{:S(2)}, u32[]{:S(2)}) collective-permute-start(bf16[2,3,16,896]{3,2,1,0:T(8,128)(2,1)S(1)} %add_convert_fusion.1), channel_id=1, source_target_pairs={{0,64},{1,65},{2,66},{3,67},{4,68},{5,69},{6,70},{7,71},{8,72},{9,... | collective-permute-start | bytes 516104 | tf_op jit(solution)/shard_map/ppermute | solution.py:42
  29.6 3.1 %collective-permute-start.19 = (bf16[1,2,16,896]{3,2,1,0:T(8,128)(2,1)S(1)}, bf16[1,2,16,896]{3,2,1,0:T(8,128)(2,1)S(1)}, u32[]{:S(2)}, u32[]{:S(2)}) collective-permute-start(bf16[1,2,16,896]{3,2,1,0:T(8,128)(2,1)S(1)} %get-tuple-element.29), channel_id=1, source_target_pairs={{0,64},{1,65},{2,66},{3,67},{4,68},{5,69},{6,70},{7,71},{8,72},{9,... | collective-permute-start | bytes 172040 | tf_op jit(solution)/shard_map/ppermute | solution.py:42
  30.6 5.6 %collective-permute-start.11 = (bf16[2,3,16,896]{3,2,1,0:T(8,128)(2,1)S(1)}, bf16[2,3,16,896]{3,2,1,0:T(8,128)(2,1)S(1)}, u32[]{:S(2)}, u32[]{:S(2)}) collective-permute-start(bf16[2,3,16,896]{3,2,1,0:T(8,128)(2,1)S(1)} %add_convert_fusion), channel_id=1, source_target_pairs={{0,192},{1,193},{2,194},{3,195},{4,196},{5,197},{6,198},{7,199},{8... | collective-permute-start | bytes 516104 | tf_op jit(solution)/shard_map/ppermute | solution.py:42
  32.8 9.6 %collective-permute-start.20 = (bf16[2,2,16,896]{3,2,1,0:T(8,128)(2,1)S(1)}, bf16[2,2,16,896]{3,2,1,0:T(8,128)(2,1)S(1)}, u32[]{:S(2)}, u32[]{:S(2)}) collective-permute-start(bf16[2,2,16,896]{3,2,1,0:T(8,128)(2,1)S(1)} %pad_maximum_fusion.11), channel_id=1, source_target_pairs={{0,32},{1,33},{2,34},{3,35},{4,36},{5,37},{6,38},{7,39},{8,40},{9,... | collective-permute-start | bytes 344072 | tf_op jit(solution)/shard_map/ppermute | solution.py:42
  34.4 4.6 %collective-permute-start.2 = (bf16[3,16,896]{2,1,0:T(8,128)(2,1)S(1)}, bf16[3,16,896]{2,1,0:T(8,128)(2,1)S(1)}, u32[]{:S(2)}, u32[]{:S(2)}) collective-permute-start(bf16[3,16,896]{2,1,0:T(8,128)(2,1)S(1)} %fusion.3), channel_id=1, source_target_pairs={{0,192},{1,193},{2,194},{3,195},{4,196},{5,197},{6,198},{7,199},{8... | collective-permute-start | bytes 258056 | tf_op jit(solution)/shard_map/ppermute | solution.py:42
  36.2 4.4 %collective-permute-start.12 = (bf16[3,16,896]{2,1,0:T(8,128)(2,1)S(1)}, bf16[3,16,896]{2,1,0:T(8,128)(2,1)S(1)}, u32[]{:S(2)}, u32[]{:S(2)}) collective-permute-start(bf16[3,16,896]{2,1,0:T(8,128)(2,1)S(1)} %fusion.5), channel_id=1, source_target_pairs={{0,32},{1,33},{2,34},{3,35},{4,36},{5,37},{6,38},{7,39},{8,40},{9,... | collective-permute-start | bytes 258056 | tf_op jit(solution)/shard_map/ppermute | solution.py:42
  39.1 4.6 %collective-permute-start.7 = (bf16[1,3,16,896]{3,2,1,0:T(8,128)(2,1)S(1)}, bf16[1,3,16,896]{3,2,1,0:T(8,128)(2,1)S(1)}, u32[]{:S(2)}, u32[]{:S(2)}) collective-permute-start(bf16[1,3,16,896]{3,2,1,0:T(8,128)(2,1)S(1)} %get-tuple-element.25), channel_id=1, source_target_pairs={{0,192},{1,193},{2,194},{3,195},{4,196},{5,197},{6,198},{7,199},{8... | collective-permute-start | bytes 258056 | tf_op jit(solution)/shard_map/ppermute | solution.py:42
  40.7 3.4 %collective-permute-start.13 = (bf16[1,3,16,896]{3,2,1,0:T(8,128)(2,1)S(1)}, bf16[1,3,16,896]{3,2,1,0:T(8,128)(2,1)S(1)}, u32[]{:S(2)}, u32[]{:S(2)}) collective-permute-start(bf16[1,3,16,896]{3,2,1,0:T(8,128)(2,1)S(1)} %get-tuple-element.27), channel_id=1, source_target_pairs={{0,32},{1,33},{2,34},{3,35},{4,36},{5,37},{6,38},{7,39},{8,40},{9,... | collective-permute-start | bytes 258056 | tf_op jit(solution)/shard_map/ppermute | solution.py:42
  42.3 6.2 %collective-permute-start.22 = (bf16[2,32,896]{2,1,0:T(8,128)(2,1)S(1)}, bf16[2,32,896]{2,1,0:T(8,128)(2,1)S(1)}, u32[]{:S(2)}, u32[]{:S(2)}) collective-permute-start(bf16[2,32,896]{2,1,0:T(8,128)(2,1)S(1)} %bitcast.51), channel_id=1, source_target_pairs={{0,2},{1,3},{2,0},{3,1},{4,6},{5,7},{6,4},{7,5},{8,10},{9,11},{10,... | collective-permute-start | bytes 344072 | tf_op jit(solution)/shard_map/ppermute | solution.py:42
  42.4 34.9 %collective-permute-start.21 = (bf16[4,2,16,896]{3,2,1,0:T(8,128)(2,1)S(1)}, bf16[4,2,16,896]{3,2,1,0:T(8,128)(2,1)S(1)}, u32[]{:S(2)}, u32[]{:S(2)}) collective-permute-start(bf16[4,2,16,896]{3,2,1,0:T(8,128)(2,1)S(1)} %pad_maximum_fusion.3.refs_2_), channel_id=1, source_target_pairs={{0,192},{1,193},{2,194},{3,195},{4,196},{5,197},{6,198},{7,199},{8... | collective-permute-start | bytes 688136 | tf_op jit(solution)/shard_map/ppermute | solution.py:42
  43.8 8.9 %collective-permute-start.8 = (bf16[2,3,16,896]{3,2,1,0:T(8,128)(2,1)S(1)}, bf16[2,3,16,896]{3,2,1,0:T(8,128)(2,1)S(1)}, u32[]{:S(2)}, u32[]{:S(2)}) collective-permute-start(bf16[2,3,16,896]{3,2,1,0:T(8,128)(2,1)S(1)} %pad_maximum_fusion.5), channel_id=1, source_target_pairs={{0,64},{1,65},{2,66},{3,67},{4,68},{5,69},{6,70},{7,71},{8,72},{9,... | collective-permute-start | bytes 516104 | tf_op jit(solution)/shard_map/ppermute | solution.py:42
  44.1 8.7 %collective-permute-start.14 = (bf16[2,3,16,896]{3,2,1,0:T(8,128)(2,1)S(1)}, bf16[2,3,16,896]{3,2,1,0:T(8,128)(2,1)S(1)}, u32[]{:S(2)}, u32[]{:S(2)}) collective-permute-start(bf16[2,3,16,896]{3,2,1,0:T(8,128)(2,1)S(1)} %pad_maximum_fusion.6), channel_id=1, source_target_pairs={{0,192},{1,193},{2,194},{3,195},{4,196},{5,197},{6,198},{7,199},{8... | collective-permute-start | bytes 516104 | tf_op jit(solution)/shard_map/ppermute | solution.py:42
  48.5 10.8 %collective-permute-start.23 = (bf16[2,2,32,896]{3,2,0,1:T(8,128)(2,1)S(1)}, bf16[2,2,32,896]{3,2,0,1:T(8,128)(2,1)S(1)}, u32[]{:S(2)}, u32[]{:S(2)}) collective-permute-start(bf16[2,2,32,896]{3,2,0,1:T(8,128)(2,1)S(1)} %pad_maximum_fusion.4), channel_id=1, source_target_pairs={{0,0},{1,21},{2,2},{3,23},{4,36},{5,49},{6,38},{7,51},{8,72},{9,93... | collective-permute-start | bytes 688136 | tf_op jit(solution)/shard_map/ppermute | solution.py:42
  52.7 24.6 %collective-permute-start.9 = (bf16[4,3,16,896]{3,2,1,0:T(8,128)(2,1)S(1)}, bf16[4,3,16,896]{3,2,1,0:T(8,128)(2,1)S(1)}, u32[]{:S(2)}, u32[]{:S(2)}) collective-permute-start(bf16[4,3,16,896]{3,2,1,0:T(8,128)(2,1)S(1)} %pad_maximum_fusion.refs_0_), channel_id=1, source_target_pairs={{0,32},{1,33},{2,34},{3,35},{4,36},{5,37},{6,38},{7,39},{8,40},{9,... | collective-permute-start | bytes 1032200 | tf_op jit(solution)/shard_map/ppermute | solution.py:42
  52.9 24.4 %collective-permute-start.15 = (bf16[4,3,16,896]{3,2,1,0:T(8,128)(2,1)S(1)}, bf16[4,3,16,896]{3,2,1,0:T(8,128)(2,1)S(1)}, u32[]{:S(2)}, u32[]{:S(2)}) collective-permute-start(bf16[4,3,16,896]{3,2,1,0:T(8,128)(2,1)S(1)} %pad_maximum_fusion.1.refs_1_), channel_id=1, source_target_pairs={{0,64},{1,65},{2,66},{3,67},{4,68},{5,69},{6,70},{7,71},{8,72},{9,... | collective-permute-start | bytes 1032200 | tf_op jit(solution)/shard_map/ppermute | solution.py:42
  59.2 17.2 %collective-permute-start.24 = (bf16[2,32,896]{2,1,0:T(8,128)(2,1)S(1)}, bf16[2,32,896]{2,1,0:T(8,128)(2,1)S(1)}, u32[]{:S(2)}, u32[]{:S(2)}) collective-permute-start(bf16[2,32,896]{2,1,0:T(8,128)(2,1)S(1)} %slice_bitcast_fusion), channel_id=1, source_target_pairs={{0,1},{1,0},{2,3},{3,2},{4,5},{5,4},{6,7},{7,6},{8,9},{9,8},{10,11... | collective-permute-start | bytes 344072 | tf_op jit(solution)/shard_map/ppermute | solution.py:42
